TPU v7x, 32 devices: a whole 2x2x4 slice. The times are simulated.
32 devices in a mesh: image: 4 (over y, x), band: 2 (over core), ga: 4 (over z).
Axes of the slice: x: 2, y: 2, z: 4, core: 2. Of those that a mesh axis runs over, the one named last changes fastest.
Arguments:
- wave_coeffs: bfloat16 [4, 64, 2, 262144], P('image', 'band', None, 'ga'), may hold values from -6 to 6
- occupation: float32 [4, 64], P('image', 'band'), may hold values from 0.003125 to 0.0625
- form_factor: float32 [4, 8, 262144], P(None, None, 'ga'), may hold values from -0.005859375 to 0.005859375
- g_vectors: float32 [3, 262144], P(None, 'ga'), may hold values from -2 to 2
- species: int32 [64], replicated, may hold values from 0 to 3
- proj_count: int32 [4], replicated, may hold values from 1 to 8, as said below
- coupling: float32 [4, 8], replicated, may hold values from 0.5 to 2.5
- positions: float32 [4, 3, 64], P('image'), may hold values from -5.4 to 29.4, as said below
- energy_rest: float32 [4], P('image'), may hold values from -8 to 8
- force_rest: float32 [4, 3, 64], P('image'), may hold values from -6 to 6
- end_positions: float32 [2, 3, 64], replicated, may hold values from -5.4 to 29.4, as said below
- end_energy: float32 [2], replicated, may hold values from -8 to 8
- climb_index: int32 [1], replicated, may hold values from 0 to 3
- tangent_kind: int32 [4], P('image'), may hold values from 0 to 3
Outputs:
- neb_force: float32 [4, 3, 64], P('image')
- energy: float32 [4], P('image')
Inputs may be any that keep to these rules, and one draw needn't show every extreme that they name: `proj_count`: each species has between 1 and 8 live projector slots, and some species has exactly 8. `positions`: atom coordinates in bohr. `end_positions`: atom coordinates in bohr.
All inputs are finite; a program needn't handle non-finite values.
Results may differ from a plain program's by a relative error of at most 0.0003.
The roundings to bfloat16 on the way count: a program that leaves them out, or rounds other values in their place, can miss the bound.
Values sent between devices are 32-bit elements; how exact they have to be, the bound alone decides.
No kernel may reach another device: no remote copies, remote signals or barrier semaphores. Data moves between devices by JAX's collectives and lax.ppermute only.
A program may use at most 128 MiB of HBM per device.

v0:
```python
import math

import jax
import jax.numpy as jnp
from jax import lax
from jax.sharding import PartitionSpec as P

ATOMS = 64
PMAX = 8
SPECIES = 4


spring_constant = 5.0


def passed_along(array, axis, by):
    length = lax.axis_size(axis)
    pairs = [(i, i + by) for i in range(length) if 0 <= i + by < length]
    return lax.ppermute(array, axis, pairs)


def atom_tables(species, proj_count, coupling):
    is_species = (species[:, None] == jnp.arange(SPECIES)[None, :]).astype(jnp.float32)
    is_live = (jnp.arange(PMAX)[None, :] < proj_count[:, None]).astype(jnp.float32)
    species_mask = is_species[:, :, None] * is_live[None, :, :]
    strength = jnp.sum(species_mask * coupling[None, :, :], axis=1)
    return (species_mask, strength)


def projectors(atom_pos, species_mask, form_factor, g_vectors):
    phases = atom_pos[0][:, None] * g_vectors[0][None, :]
    phases = phases + atom_pos[1][:, None] * g_vectors[1][None, :]
    phases = phases + atom_pos[2][:, None] * g_vectors[2][None, :]
    cosine = jnp.cos(phases)
    sine_part = jnp.sin(phases)
    radial = species_mask[:, 0, :, None] * form_factor[0][None, :, :]
    for spec_num in range(1, SPECIES):
        radial = radial + species_mask[:, spec_num, :, None] * form_factor[spec_num][None, :, :]
    real_part = radial * cosine[:, None, :]
    imag_part = -radial * sine_part[:, None, :]
    joined = jnp.concatenate([real_part, imag_part], axis=-1).astype(jnp.bfloat16)
    return joined.reshape(joined.shape[0] * joined.shape[1], joined.shape[2])


def stack_waves(waves_here, g_vectors):
    band_count = waves_here.shape[0]
    real_part = waves_here[:, 0, :].astype(jnp.float32)
    imag_part = waves_here[:, 1, :].astype(jnp.float32)
    pieces = [waves_here.reshape(band_count, 2 * waves_here.shape[2])]
    for axis_num in range(3):
        direction = g_vectors[axis_num][None, :]
        pieces.append(
            jnp.concatenate([-direction * imag_part, direction * real_part], axis=-1).astype(
                jnp.bfloat16
            )
        )
    return jnp.concatenate(pieces, axis=0)


def contract(projector, stacked):
    return 2.0 * lax.dot_general(
        projector, stacked, (((1,), (1,)), ((), ())), preferred_element_type=jnp.float32
    )


def nonlocal_terms(proj_sums, occupied, strength):
    band_count = occupied.shape[0]
    atom_count = strength.shape[0]
    intersect = proj_sums[:, :band_count]
    weighted = intersect * occupied[None, :]
    energy_part = jnp.sum(strength.reshape(-1) * jnp.sum(weighted * intersect, axis=1))
    forces = []
    for axis_num in range(3):
        slope = proj_sums[:, (axis_num + 1) * band_count : (axis_num + 2) * band_count]
        per_row = jnp.sum(weighted * slope, axis=1).reshape(atom_count, PMAX)
        forces.append(-2.0 * jnp.sum(strength * per_row, axis=1))
    return (energy_part, jnp.stack(forces, axis=0))


def neb_project(
    force, here, prev_pos, next_pos, energy, prev_energy, next_energy, tangent_kind, is_climb
):
    to_next = next_pos - here
    from_prev = here - prev_pos
    rise_next = jnp.abs(next_energy - energy)
    rise_prev = jnp.abs(prev_energy - energy)
    larger = jnp.maximum(rise_next, rise_prev)
    smaller = jnp.minimum(rise_next, rise_prev)
    rising = next_energy > prev_energy
    weight_next = 1.0 + jnp.where(rising, larger, smaller)
    weight_prev = 1.0 + jnp.where(rising, smaller, larger)
    stiff_next = spring_constant * (1.0 + jax.nn.sigmoid(0.5 * (next_energy + energy)))
    stiff_prev = spring_constant * (1.0 + jax.nn.sigmoid(0.5 * (prev_energy + energy)))
    length_next = jnp.sqrt(jnp.sum(to_next * to_next, axis=(1, 2)) + 1.0)
    length_prev = jnp.sqrt(jnp.sum(from_prev * from_prev, axis=(1, 2)) + 1.0)
    upwind = weight_next[:, None, None] * to_next + weight_prev[:, None, None] * from_prev
    forward = to_next / length_next[:, None, None]
    backward = from_prev / length_prev[:, None, None]
    kind = tangent_kind[:, None, None]
    tangent = jnp.where(
        kind == 0,
        upwind,
        jnp.where(kind == 1, forward + backward, jnp.where(kind == 2, forward, backward)),
    )
    unit_tangent = tangent / jnp.sqrt(jnp.sum(tangent * tangent, axis=(1, 2)) + 1.0)[:, None, None]
    along = jnp.sum(force * unit_tangent, axis=(1, 2))[:, None, None]
    climbing = force - 2.0 * along * unit_tangent
    regular = (
        force
        - along * unit_tangent
        + (stiff_next * length_next - stiff_prev * length_prev)[:, None, None] * unit_tangent
    )
    return jnp.where(is_climb[:, None, None], climbing, regular)


def per_device(
    wave_coeffs,
    occupation,
    form_factor,
    g_vectors,
    species,
    proj_count,
    coupling,
    positions,
    energy_rest,
    force_rest,
    end_positions,
    end_energy,
    climb_index,
    tangent_kind,
):
    species_mask, strength = atom_tables(species, proj_count, coupling)
    stacked = stack_waves(wave_coeffs[0], g_vectors)
    atom_pos = positions[0]
    occupied = occupation[0]
    local_atoms = ATOMS // lax.axis_size("ga")
    natoms = lax.axis_size("ga") * (local_atoms * PMAX) // PMAX
    block_atoms = math.gcd(natoms, 8)
    block_count = natoms // block_atoms

    def one_block(block_num):
        begin = block_num * block_atoms
        pos_part = lax.dynamic_slice_in_dim(atom_pos, begin, block_atoms, 1)
        mask_part = lax.dynamic_slice_in_dim(species_mask, begin, block_atoms, 0)
        projector = projectors(pos_part, mask_part, form_factor, g_vectors)
        return contract(projector, stacked)

    blocks = lax.map(one_block, jnp.arange(block_count, dtype=jnp.int32))
    proj_sums = lax.psum_scatter(
        blocks.reshape(lax.axis_size("ga") * (local_atoms * PMAX), blocks.shape[2]),
        "ga",
        scatter_dimension=0,
        tiled=True,
    )
    first_local = lax.axis_index("ga") * local_atoms
    strength_part = lax.dynamic_slice_in_dim(strength, first_local, local_atoms, 0)
    energy_part, force_part = nonlocal_terms(proj_sums, occupied, strength_part)
    force_full = lax.dynamic_update_slice_in_dim(
        jnp.zeros((3, ATOMS), jnp.float32), force_part, first_local, 1
    )
    force_nl, energy_nl = lax.psum((force_full, energy_part), ("band", "ga"))
    energy = energy_rest + energy_nl
    force = force_rest + force_nl[None, :, :]
    image_index = lax.axis_index("image")
    image_count = lax.axis_size("image")
    prev_pos, prev_energy = passed_along((positions, energy), "image", 1)
    next_pos, next_energy = passed_along((positions, energy), "image", -1)
    at_start = image_index == 0
    at_end = image_index == image_count - 1
    prev_pos = jnp.where(at_start, end_positions[:1], prev_pos)
    prev_energy = jnp.where(at_start, end_energy[:1], prev_energy)
    next_pos = jnp.where(at_end, end_positions[1:], next_pos)
    next_energy = jnp.where(at_end, end_energy[1:], next_energy)
    is_climb = climb_index == image_index
    neb_force = neb_project(
        force,
        positions,
        prev_pos,
        next_pos,
        energy,
        prev_energy,
        next_energy,
        tangent_kind,
        is_climb,
    )
    return (neb_force, energy)


def solution(mesh):
    in_specs = (
        P("image", "band", None, "ga"),
        P("image", "band"),
        P(None, None, "ga"),
        P(None, "ga"),
        P(),
        P(),
        P(),
        P("image", None, None),
        P("image"),
        P("image", None, None),
        P(),
        P(),
        P(),
        P("image"),
    )
    out_specs = (P("image", None, None), P("image"))
    return jax.shard_map(
        per_device, mesh=mesh, in_specs=in_specs, out_specs=out_specs, check_vma=False
    )
```

profile of v0, /device:TPU:0, one launch (start us, length us, event | category | flops | bytes accessed | tf_op | source)
XLA Modules:
  0.0 495.8 jit_solution(12837943678773757339)
XLA Ops:
  10.5 11.2 %copy.24 = bf16[1,32,2,65536]{3,1,2,0:T(8,128)(2,1)} copy(bf16[1,32,2,65536]{3,2,1,0:T(2,128)(2,1)} %param.16) | data formatting | bytes 16777216 | tf_op args[0]
  21.7 11.2 %copy.21 = bf16[4,8,2,65536]{3,1,2,0:T(8,128)(2,1)} copy(bf16[4,8,2,65536]{3,2,1,0:T(2,128)(2,1)} %bitcast.165) | data formatting | bytes 16777216
  33.7 11.5 %fusion.22 = (bf16[32,65536]{1,0:T(8,128)(2,1)}, bf16[32,65536]{1,0:T(8,128)(2,1)}, bf16[32,65536]{1,0:T(8,128)(2,1)}, bf16[32,65536]{1,0:T(8,128)(2,1)}, bf16[3...) fusion(f32[65536]{0:T(1024)S(1)} %bitcast.171, bf16[32,2,65536]{2,0,1:T(8,128)(2,1)} %bitcast.166, f32[65536]{0:T(1024)S(1)} %bitcast.176, ...), kind=kLoop, calls=%fused_computation.42 | loop fusion | flops 29360128 | bytes 35127296 | tf_op jit(solution)/shard_map/convert.8
  45.3 32.5 %maximum_maximum_fusion = bf16[128,131072]{1,0:T(8,128)(2,1)} fusion(bf16[32,65536]{1,0:T(8,128)(2,1)} %get-tuple-element.99, bf16[32,65536]{1,0:T(8,128)(2,1)} %get-tuple-element.101, bf16[32,65536]{1,0:T(8,128)(2,1)} %get-tuple-element.100, bf16[32,65536]{1,0:T(8,128)(2,1)} %get-tuple-element.102, bf16[32,65536]{1,0:T(8,128)(2,1)} %get-tuple-element.103, ...), kind=kLoop, calls=%fused_computation.35 | loop fusion | flops 234881024 | bytes 67108864 | tf_op jit(solution)/shard_map/concatenate | solution.py:57
  77.8 351.9 %while.10 = (s32[]{:T(128)}, f32[8,64,128]{2,1,0:T(8,128)S(1)}, s32[8]{0:T(128)S(1)}, f32[64,4,8]{2,0,1:T(8,128)S(1)}, f32[4,8,65536]{2,1,0:T(8,128)}, /*index=5...) while((s32[]{:T(128)}, f32[8,64,128]{2,1,0:T(8,128)S(1)}, ...), condition=%wide.region_2.3_spmd, body=%wide.region_1.2_spmd.sunk | while | flops 2233999360 | bytes 111457432 | solution.py:148
  79.7 8.6 %fusion.50 = (f32[8,65536]{1,0:T(8,128)S(1)}, f32[8,65536]{1,0:T(8,128)}) fusion(f32[65536]{0:T(1024)S(1)} %bitcast.169, f32[8]{0:T(128)S(1)} %get-tuple-element.186, f32[65536]{0:T(1024)S(1)} %bitcast.170, f32[8]{0:T(128)S(1)} %get-tuple-element.188, f32[65536]{0:T(1024)S(1)} %bitcast.168, f32[8]{0:T(128)S(1)} %get-tuple-element.190), kind=kLoop, calls=%fused_computation.18.clone.1 | loop fusion | flops 2621440 | bytes 4980832 | tf_op jit(solution)/shard_map/while/body/eval_jaxpr/cos | solution.py:34
  93.4 8.9 %fusion.51 = (bf16[64,65536]{1,0:T(8,128)(2,1)}, bf16[64,65536]{1,0:T(8,128)(2,1)}) fusion(f32[8,65536]{1,0:T(8,128)S(1)} %get-tuple-element.191, f32[8,65536]{1,0:T(8,128)S(1)} %get-tuple-element.192, f32[64]{0:T(128)S(1)} %copy-done.5, f32[8,65536]{1,0:T(8,128)S(1)} %get-tuple-element.194, f32[64]{0:T(128)S(1)} %mul.729, ...), kind=kLoop, calls=%fused_computation.7.clone.1 | loop fusion | flops 50331648 | bytes 29361152 | tf_op jit(solution)/shard_map/convert
  102.3 19.5 %fusion.52 = f32[8,64,128]{2,1,0:T(8,128)S(1)} fusion(f32[8,64,128]{2,1,0:T(8,128)S(1)} %get-tuple-element.219, s32[]{:T(128)} %get-tuple-element.218, bf16[128,131072]{1,0:T(8,128)(2,1)} %get-tuple-element.240, bf16[64,65536]{1,0:T(8,128)(2,1)} %get-tuple-element.201, bf16[64,65536]{1,0:T(8,128)(2,1)} %get-tuple-element.202), kind=kOutput, calls=%fused_computation.25.clone.1 | convolution fusion | flops 2181046272 | bytes 50364420 | tf_op jit(solution)/shard_map/while/body/eval_jaxpr/dot_general | solution.py:61
  123.7 8.6 %fusion.50 = (f32[8,65536]{1,0:T(8,128)S(1)}, f32[8,65536]{1,0:T(8,128)}) fusion(f32[65536]{0:T(1024)S(1)} %bitcast.169, f32[8]{0:T(128)S(1)} %get-tuple-element.186, f32[65536]{0:T(1024)S(1)} %bitcast.170, f32[8]{0:T(128)S(1)} %get-tuple-element.188, f32[65536]{0:T(1024)S(1)} %bitcast.168, f32[8]{0:T(128)S(1)} %get-tuple-element.190), kind=kLoop, calls=%fused_computation.18.clone.1 | loop fusion | flops 2621440 | bytes 4980832 | tf_op jit(solution)/shard_map/while/body/eval_jaxpr/cos | solution.py:34
  137.4 8.9 %fusion.51 = (bf16[64,65536]{1,0:T(8,128)(2,1)}, bf16[64,65536]{1,0:T(8,128)(2,1)}) fusion(f32[8,65536]{1,0:T(8,128)S(1)} %get-tuple-element.191, f32[8,65536]{1,0:T(8,128)S(1)} %get-tuple-element.192, f32[64]{0:T(128)S(1)} %copy-done.5, f32[8,65536]{1,0:T(8,128)S(1)} %get-tuple-element.194, f32[64]{0:T(128)S(1)} %mul.729, ...), kind=kLoop, calls=%fused_computation.7.clone.1 | loop fusion | flops 50331648 | bytes 29361152 | tf_op jit(solution)/shard_map/convert
  146.3 19.5 %fusion.52 = f32[8,64,128]{2,1,0:T(8,128)S(1)} fusion(f32[8,64,128]{2,1,0:T(8,128)S(1)} %get-tuple-element.219, s32[]{:T(128)} %get-tuple-element.218, bf16[128,131072]{1,0:T(8,128)(2,1)} %get-tuple-element.240, bf16[64,65536]{1,0:T(8,128)(2,1)} %get-tuple-element.201, bf16[64,65536]{1,0:T(8,128)(2,1)} %get-tuple-element.202), kind=kOutput, calls=%fused_computation.25.clone.1 | convolution fusion | flops 2181046272 | bytes 50364420 | tf_op jit(solution)/shard_map/while/body/eval_jaxpr/dot_general | solution.py:61
  167.7 8.6 %fusion.50 = (f32[8,65536]{1,0:T(8,128)S(1)}, f32[8,65536]{1,0:T(8,128)}) fusion(f32[65536]{0:T(1024)S(1)} %bitcast.169, f32[8]{0:T(128)S(1)} %get-tuple-element.186, f32[65536]{0:T(1024)S(1)} %bitcast.170, f32[8]{0:T(128)S(1)} %get-tuple-element.188, f32[65536]{0:T(1024)S(1)} %bitcast.168, f32[8]{0:T(128)S(1)} %get-tuple-element.190), kind=kLoop, calls=%fused_computation.18.clone.1 | loop fusion | flops 2621440 | bytes 4980832 | tf_op jit(solution)/shard_map/while/body/eval_jaxpr/cos | solution.py:34
  181.4 8.9 %fusion.51 = (bf16[64,65536]{1,0:T(8,128)(2,1)}, bf16[64,65536]{1,0:T(8,128)(2,1)}) fusion(f32[8,65536]{1,0:T(8,128)S(1)} %get-tuple-element.191, f32[8,65536]{1,0:T(8,128)S(1)} %get-tuple-element.192, f32[64]{0:T(128)S(1)} %copy-done.5, f32[8,65536]{1,0:T(8,128)S(1)} %get-tuple-element.194, f32[64]{0:T(128)S(1)} %mul.729, ...), kind=kLoop, calls=%fused_computation.7.clone.1 | loop fusion | flops 50331648 | bytes 29361152 | tf_op jit(solution)/shard_map/convert
  190.3 19.5 %fusion.52 = f32[8,64,128]{2,1,0:T(8,128)S(1)} fusion(f32[8,64,128]{2,1,0:T(8,128)S(1)} %get-tuple-element.219, s32[]{:T(128)} %get-tuple-element.218, bf16[128,131072]{1,0:T(8,128)(2,1)} %get-tuple-element.240, bf16[64,65536]{1,0:T(8,128)(2,1)} %get-tuple-element.201, bf16[64,65536]{1,0:T(8,128)(2,1)} %get-tuple-element.202), kind=kOutput, calls=%fused_computation.25.clone.1 | convolution fusion | flops 2181046272 | bytes 50364420 | tf_op jit(solution)/shard_map/while/body/eval_jaxpr/dot_general | solution.py:61
  211.7 8.6 %fusion.50 = (f32[8,65536]{1,0:T(8,128)S(1)}, f32[8,65536]{1,0:T(8,128)}) fusion(f32[65536]{0:T(1024)S(1)} %bitcast.169, f32[8]{0:T(128)S(1)} %get-tuple-element.186, f32[65536]{0:T(1024)S(1)} %bitcast.170, f32[8]{0:T(128)S(1)} %get-tuple-element.188, f32[65536]{0:T(1024)S(1)} %bitcast.168, f32[8]{0:T(128)S(1)} %get-tuple-element.190), kind=kLoop, calls=%fused_computation.18.clone.1 | loop fusion | flops 2621440 | bytes 4980832 | tf_op jit(solution)/shard_map/while/body/eval_jaxpr/cos | solution.py:34
  225.4 8.9 %fusion.51 = (bf16[64,65536]{1,0:T(8,128)(2,1)}, bf16[64,65536]{1,0:T(8,128)(2,1)}) fusion(f32[8,65536]{1,0:T(8,128)S(1)} %get-tuple-element.191, f32[8,65536]{1,0:T(8,128)S(1)} %get-tuple-element.192, f32[64]{0:T(128)S(1)} %copy-done.5, f32[8,65536]{1,0:T(8,128)S(1)} %get-tuple-element.194, f32[64]{0:T(128)S(1)} %mul.729, ...), kind=kLoop, calls=%fused_computation.7.clone.1 | loop fusion | flops 50331648 | bytes 29361152 | tf_op jit(solution)/shard_map/convert
  234.3 19.5 %fusion.52 = f32[8,64,128]{2,1,0:T(8,128)S(1)} fusion(f32[8,64,128]{2,1,0:T(8,128)S(1)} %get-tuple-element.219, s32[]{:T(128)} %get-tuple-element.218, bf16[128,131072]{1,0:T(8,128)(2,1)} %get-tuple-element.240, bf16[64,65536]{1,0:T(8,128)(2,1)} %get-tuple-element.201, bf16[64,65536]{1,0:T(8,128)(2,1)} %get-tuple-element.202), kind=kOutput, calls=%fused_computation.25.clone.1 | convolution fusion | flops 2181046272 | bytes 50364420 | tf_op jit(solution)/shard_map/while/body/eval_jaxpr/dot_general | solution.py:61
  255.7 8.6 %fusion.50 = (f32[8,65536]{1,0:T(8,128)S(1)}, f32[8,65536]{1,0:T(8,128)}) fusion(f32[65536]{0:T(1024)S(1)} %bitcast.169, f32[8]{0:T(128)S(1)} %get-tuple-element.186, f32[65536]{0:T(1024)S(1)} %bitcast.170, f32[8]{0:T(128)S(1)} %get-tuple-element.188, f32[65536]{0:T(1024)S(1)} %bitcast.168, f32[8]{0:T(128)S(1)} %get-tuple-element.190), kind=kLoop, calls=%fused_computation.18.clone.1 | loop fusion | flops 2621440 | bytes 4980832 | tf_op jit(solution)/shard_map/while/body/eval_jaxpr/cos | solution.py:34
  269.4 8.9 %fusion.51 = (bf16[64,65536]{1,0:T(8,128)(2,1)}, bf16[64,65536]{1,0:T(8,128)(2,1)}) fusion(f32[8,65536]{1,0:T(8,128)S(1)} %get-tuple-element.191, f32[8,65536]{1,0:T(8,128)S(1)} %get-tuple-element.192, f32[64]{0:T(128)S(1)} %copy-done.5, f32[8,65536]{1,0:T(8,128)S(1)} %get-tuple-element.194, f32[64]{0:T(128)S(1)} %mul.729, ...), kind=kLoop, calls=%fused_computation.7.clone.1 | loop fusion | flops 50331648 | bytes 29361152 | tf_op jit(solution)/shard_map/convert
  278.3 19.5 %fusion.52 = f32[8,64,128]{2,1,0:T(8,128)S(1)} fusion(f32[8,64,128]{2,1,0:T(8,128)S(1)} %get-tuple-element.219, s32[]{:T(128)} %get-tuple-element.218, bf16[128,131072]{1,0:T(8,128)(2,1)} %get-tuple-element.240, bf16[64,65536]{1,0:T(8,128)(2,1)} %get-tuple-element.201, bf16[64,65536]{1,0:T(8,128)(2,1)} %get-tuple-element.202), kind=kOutput, calls=%fused_computation.25.clone.1 | convolution fusion | flops 2181046272 | bytes 50364420 | tf_op jit(solution)/shard_map/while/body/eval_jaxpr/dot_general | solution.py:61
  299.7 8.6 %fusion.50 = (f32[8,65536]{1,0:T(8,128)S(1)}, f32[8,65536]{1,0:T(8,128)}) fusion(f32[65536]{0:T(1024)S(1)} %bitcast.169, f32[8]{0:T(128)S(1)} %get-tuple-element.186, f32[65536]{0:T(1024)S(1)} %bitcast.170, f32[8]{0:T(128)S(1)} %get-tuple-element.188, f32[65536]{0:T(1024)S(1)} %bitcast.168, f32[8]{0:T(128)S(1)} %get-tuple-element.190), kind=kLoop, calls=%fused_computation.18.clone.1 | loop fusion | flops 2621440 | bytes 4980832 | tf_op jit(solution)/shard_map/while/body/eval_jaxpr/cos | solution.py:34
  313.3 8.9 %fusion.51 = (bf16[64,65536]{1,0:T(8,128)(2,1)}, bf16[64,65536]{1,0:T(8,128)(2,1)}) fusion(f32[8,65536]{1,0:T(8,128)S(1)} %get-tuple-element.191, f32[8,65536]{1,0:T(8,128)S(1)} %get-tuple-element.192, f32[64]{0:T(128)S(1)} %copy-done.5, f32[8,65536]{1,0:T(8,128)S(1)} %get-tuple-element.194, f32[64]{0:T(128)S(1)} %mul.729, ...), kind=kLoop, calls=%fused_computation.7.clone.1 | loop fusion | flops 50331648 | bytes 29361152 | tf_op jit(solution)/shard_map/convert
  322.3 19.5 %fusion.52 = f32[8,64,128]{2,1,0:T(8,128)S(1)} fusion(f32[8,64,128]{2,1,0:T(8,128)S(1)} %get-tuple-element.219, s32[]{:T(128)} %get-tuple-element.218, bf16[128,131072]{1,0:T(8,128)(2,1)} %get-tuple-element.240, bf16[64,65536]{1,0:T(8,128)(2,1)} %get-tuple-element.201, bf16[64,65536]{1,0:T(8,128)(2,1)} %get-tuple-element.202), kind=kOutput, calls=%fused_computation.25.clone.1 | convolution fusion | flops 2181046272 | bytes 50364420 | tf_op jit(solution)/shard_map/while/body/eval_jaxpr/dot_general | solution.py:61
  343.7 8.6 %fusion.50 = (f32[8,65536]{1,0:T(8,128)S(1)}, f32[8,65536]{1,0:T(8,128)}) fusion(f32[65536]{0:T(1024)S(1)} %bitcast.169, f32[8]{0:T(128)S(1)} %get-tuple-element.186, f32[65536]{0:T(1024)S(1)} %bitcast.170, f32[8]{0:T(128)S(1)} %get-tuple-element.188, f32[65536]{0:T(1024)S(1)} %bitcast.168, f32[8]{0:T(128)S(1)} %get-tuple-element.190), kind=kLoop, calls=%fused_computation.18.clone.1 | loop fusion | flops 2621440 | bytes 4980832 | tf_op jit(solution)/shard_map/while/body/eval_jaxpr/cos | solution.py:34
  357.3 8.9 %fusion.51 = (bf16[64,65536]{1,0:T(8,128)(2,1)}, bf16[64,65536]{1,0:T(8,128)(2,1)}) fusion(f32[8,65536]{1,0:T(8,128)S(1)} %get-tuple-element.191, f32[8,65536]{1,0:T(8,128)S(1)} %get-tuple-element.192, f32[64]{0:T(128)S(1)} %copy-done.5, f32[8,65536]{1,0:T(8,128)S(1)} %get-tuple-element.194, f32[64]{0:T(128)S(1)} %mul.729, ...), kind=kLoop, calls=%fused_computation.7.clone.1 | loop fusion | flops 50331648 | bytes 29361152 | tf_op jit(solution)/shard_map/convert
  366.2 19.5 %fusion.52 = f32[8,64,128]{2,1,0:T(8,128)S(1)} fusion(f32[8,64,128]{2,1,0:T(8,128)S(1)} %get-tuple-element.219, s32[]{:T(128)} %get-tuple-element.218, bf16[128,131072]{1,0:T(8,128)(2,1)} %get-tuple-element.240, bf16[64,65536]{1,0:T(8,128)(2,1)} %get-tuple-element.201, bf16[64,65536]{1,0:T(8,128)(2,1)} %get-tuple-element.202), kind=kOutput, calls=%fused_computation.25.clone.1 | convolution fusion | flops 2181046272 | bytes 50364420 | tf_op jit(solution)/shard_map/while/body/eval_jaxpr/dot_general | solution.py:61
  387.7 8.6 %fusion.50 = (f32[8,65536]{1,0:T(8,128)S(1)}, f32[8,65536]{1,0:T(8,128)}) fusion(f32[65536]{0:T(1024)S(1)} %bitcast.169, f32[8]{0:T(128)S(1)} %get-tuple-element.186, f32[65536]{0:T(1024)S(1)} %bitcast.170, f32[8]{0:T(128)S(1)} %get-tuple-element.188, f32[65536]{0:T(1024)S(1)} %bitcast.168, f32[8]{0:T(128)S(1)} %get-tuple-element.190), kind=kLoop, calls=%fused_computation.18.clone.1 | loop fusion | flops 2621440 | bytes 4980832 | tf_op jit(solution)/shard_map/while/body/eval_jaxpr/cos | solution.py:34
  401.3 8.9 %fusion.51 = (bf16[64,65536]{1,0:T(8,128)(2,1)}, bf16[64,65536]{1,0:T(8,128)(2,1)}) fusion(f32[8,65536]{1,0:T(8,128)S(1)} %get-tuple-element.191, f32[8,65536]{1,0:T(8,128)S(1)} %get-tuple-element.192, f32[64]{0:T(128)S(1)} %copy-done.5, f32[8,65536]{1,0:T(8,128)S(1)} %get-tuple-element.194, f32[64]{0:T(128)S(1)} %mul.729, ...), kind=kLoop, calls=%fused_computation.7.clone.1 | loop fusion | flops 50331648 | bytes 29361152 | tf_op jit(solution)/shard_map/convert
  410.2 19.5 %fusion.52 = f32[8,64,128]{2,1,0:T(8,128)S(1)} fusion(f32[8,64,128]{2,1,0:T(8,128)S(1)} %get-tuple-element.219, s32[]{:T(128)} %get-tuple-element.218, bf16[128,131072]{1,0:T(8,128)(2,1)} %get-tuple-element.240, bf16[64,65536]{1,0:T(8,128)(2,1)} %get-tuple-element.201, bf16[64,65536]{1,0:T(8,128)(2,1)} %get-tuple-element.202), kind=kOutput, calls=%fused_computation.25.clone.1 | convolution fusion | flops 2181046272 | bytes 50364420 | tf_op jit(solution)/shard_map/while/body/eval_jaxpr/dot_general | solution.py:61
  431.8 5.5 %collective-permute-start.3 = (f32[1,3,64]{2,0,1:T(1,128)}, f32[1,3,64]{2,0,1:T(1,128)S(1)}, u32[]{:S(2)}, u32[]{:S(2)}) collective-permute-start(f32[1,3,64]{2,0,1:T(1,128)} %param.23), channel_id=1, source_target_pairs={{0,8},{8,16},{16,24},{1,9},{9,17},{17,25},{2,10},{10,18},{18,26},{... | collective-permute-start | bytes 2312 | tf_op jit(solution)/shard_map/ppermute | solution.py:19
  443.3 10.0 %reduce-scatter.2.cloned.1.call-done = f32[128,128]{1,0:T(8,128)} async-done(((f32[512,128]{1,0:T(8,128)}), f32[128,128]{1,0:T(8,128)}) %reduce-scatter.2.cloned.1.call-update) | async-done | bytes 65552 | tf_op jit(solution)/shard_map/reduce_scatter | solution.py:149
  456.5 14.3 %all-reduce = (f32[1]{0:T(128)}, f32[1,3,64]{2,0,1:T(1,128)S(1)}) all-reduce(f32[1]{0:T(128)} %bitcast.39, f32[1,3,64]{2,0,1:T(1,128)S(1)} %dynamic_update_slice.8), channel_id=1, replica_groups=mesh['image'=4,'band'=2,'ga'=4] {'band','ga'}, use_global_device_ids=true, to_apply=%region_13.14 | all-reduce | flops 193 | bytes 1544 | tf_op jit(solution)/shard_map/psum | solution.py:161
  (221 shorter events, 73.8 us)
Async XLA Ops:
  7.2 446.2 %reduce-scatter.2.cloned.1.call-start = ((), (), s32[]{:S(2)}) async-start(), calls=%async_computation.1 | async-start | bytes 327680 | tf_op jit(solution)/shard_map/reduce_scatter | solution.py:149
  21.7 11.2 %copy-start.8 = (s32[64]{0:T(128)S(1)}, s32[64]{0:T(128)}, u32[]{:S(2)}) copy-start(s32[64]{0:T(128)} %param.20) | copy-start | bytes 772
  21.7 11.3 %copy-start.9 = (s32[4]{0:T(128)S(1)}, s32[4]{0:T(128)}, u32[]{:S(2)}) copy-start(s32[4]{0:T(128)} %param.21) | copy-start | bytes 52
  21.7 11.3 %copy-start.6 = (f32[1,3,64]{2,0,1:T(1,128)S(1)}, f32[1,3,64]{2,0,1:T(1,128)}, u32[]{:S(2)}) copy-start(f32[1,3,64]{2,0,1:T(1,128)} %param.23) | copy-start | bytes 2308
  21.7 11.3 %copy-start.7 = (f32[4,8]{1,0:T(4,128)S(1)}, f32[4,8]{1,0:T(4,128)}, u32[]{:S(2)}) copy-start(f32[4,8]{1,0:T(4,128)} %param.22) | copy-start | bytes 388
  45.3 32.6 %copy-start.1 = (f32[3,65536]{1,0:T(4,128)S(1)}, f32[3,65536]{1,0:T(4,128)}, u32[]{:S(2)}) copy-start(f32[3,65536]{1,0:T(4,128)} %param.19) | copy-start | bytes 2359300
  77.8 10.5 %copy-start.3 = (f32[3,64]{1,0:T(4,128)}, f32[3,64]{1,0:T(4,128)S(1)}, u32[]{:S(2)}) copy-start(f32[3,64]{1,0:T(4,128)S(1)} %get-tuple-element.238) | copy-start | bytes 2308 | tf_op jit(solution)/shard_map/while
  102.3 19.5 %copy-start.4 = (f32[3,64]{1,0:T(4,128)S(1)}, f32[3,64]{1,0:T(4,128)}, u32[]{:S(2)}) copy-start(f32[3,64]{1,0:T(4,128)} %copy-done.3) | copy-start | bytes 2308 | tf_op jit(solution)/shard_map/while
  102.3 19.5 %copy-start.11 = (s32[8]{0:T(128)S(1)}, s32[8]{0:T(128)}, u32[]{:S(2)}) copy-start(s32[8]{0:T(128)} %copy-done.10) | copy-start | bytes 100 | tf_op jit(solution)/shard_map/while
  121.8 10.5 %copy-start.3 = (f32[3,64]{1,0:T(4,128)}, f32[3,64]{1,0:T(4,128)S(1)}, u32[]{:S(2)}) copy-start(f32[3,64]{1,0:T(4,128)S(1)} %get-tuple-element.238) | copy-start | bytes 2308 | tf_op jit(solution)/shard_map/while
  146.3 19.5 %copy-start.4 = (f32[3,64]{1,0:T(4,128)S(1)}, f32[3,64]{1,0:T(4,128)}, u32[]{:S(2)}) copy-start(f32[3,64]{1,0:T(4,128)} %copy-done.3) | copy-start | bytes 2308 | tf_op jit(solution)/shard_map/while
  146.3 19.5 %copy-start.11 = (s32[8]{0:T(128)S(1)}, s32[8]{0:T(128)}, u32[]{:S(2)}) copy-start(s32[8]{0:T(128)} %copy-done.10) | copy-start | bytes 100 | tf_op jit(solution)/shard_map/while
  190.3 19.5 %copy-start.4 = (f32[3,64]{1,0:T(4,128)S(1)}, f32[3,64]{1,0:T(4,128)}, u32[]{:S(2)}) copy-start(f32[3,64]{1,0:T(4,128)} %copy-done.3) | copy-start | bytes 2308 | tf_op jit(solution)/shard_map/while
  190.3 19.5 %copy-start.11 = (s32[8]{0:T(128)S(1)}, s32[8]{0:T(128)}, u32[]{:S(2)}) copy-start(s32[8]{0:T(128)} %copy-done.10) | copy-start | bytes 100 | tf_op jit(solution)/shard_map/while
  209.8 10.5 %copy-start.3 = (f32[3,64]{1,0:T(4,128)}, f32[3,64]{1,0:T(4,128)S(1)}, u32[]{:S(2)}) copy-start(f32[3,64]{1,0:T(4,128)S(1)} %get-tuple-element.238) | copy-start | bytes 2308 | tf_op jit(solution)/shard_map/while
  234.3 19.5 %copy-start.4 = (f32[3,64]{1,0:T(4,128)S(1)}, f32[3,64]{1,0:T(4,128)}, u32[]{:S(2)}) copy-start(f32[3,64]{1,0:T(4,128)} %copy-done.3) | copy-start | bytes 2308 | tf_op jit(solution)/shard_map/while
  234.3 19.5 %copy-start.11 = (s32[8]{0:T(128)S(1)}, s32[8]{0:T(128)}, u32[]{:S(2)}) copy-start(s32[8]{0:T(128)} %copy-done.10) | copy-start | bytes 100 | tf_op jit(solution)/shard_map/while
  253.8 10.5 %copy-start.3 = (f32[3,64]{1,0:T(4,128)}, f32[3,64]{1,0:T(4,128)S(1)}, u32[]{:S(2)}) copy-start(f32[3,64]{1,0:T(4,128)S(1)} %get-tuple-element.238) | copy-start | bytes 2308 | tf_op jit(solution)/shard_map/while
  278.3 19.5 %copy-start.4 = (f32[3,64]{1,0:T(4,128)S(1)}, f32[3,64]{1,0:T(4,128)}, u32[]{:S(2)}) copy-start(f32[3,64]{1,0:T(4,128)} %copy-done.3) | copy-start | bytes 2308 | tf_op jit(solution)/shard_map/while
  278.3 19.5 %copy-start.11 = (s32[8]{0:T(128)S(1)}, s32[8]{0:T(128)}, u32[]{:S(2)}) copy-start(s32[8]{0:T(128)} %copy-done.10) | copy-start | bytes 100 | tf_op jit(solution)/shard_map/while
  322.3 19.5 %copy-start.4 = (f32[3,64]{1,0:T(4,128)S(1)}, f32[3,64]{1,0:T(4,128)}, u32[]{:S(2)}) copy-start(f32[3,64]{1,0:T(4,128)} %copy-done.3) | copy-start | bytes 2308 | tf_op jit(solution)/shard_map/while
  322.3 19.5 %copy-start.11 = (s32[8]{0:T(128)S(1)}, s32[8]{0:T(128)}, u32[]{:S(2)}) copy-start(s32[8]{0:T(128)} %copy-done.10) | copy-start | bytes 100 | tf_op jit(solution)/shard_map/while
  341.8 10.5 %copy-start.3 = (f32[3,64]{1,0:T(4,128)}, f32[3,64]{1,0:T(4,128)S(1)}, u32[]{:S(2)}) copy-start(f32[3,64]{1,0:T(4,128)S(1)} %get-tuple-element.238) | copy-start | bytes 2308 | tf_op jit(solution)/shard_map/while
  366.2 19.5 %copy-start.4 = (f32[3,64]{1,0:T(4,128)S(1)}, f32[3,64]{1,0:T(4,128)}, u32[]{:S(2)}) copy-start(f32[3,64]{1,0:T(4,128)} %copy-done.3) | copy-start | bytes 2308 | tf_op jit(solution)/shard_map/while
  366.2 19.5 %copy-start.11 = (s32[8]{0:T(128)S(1)}, s32[8]{0:T(128)}, u32[]{:S(2)}) copy-start(s32[8]{0:T(128)} %copy-done.10) | copy-start | bytes 100 | tf_op jit(solution)/shard_map/while
  385.8 10.5 %copy-start.3 = (f32[3,64]{1,0:T(4,128)}, f32[3,64]{1,0:T(4,128)S(1)}, u32[]{:S(2)}) copy-start(f32[3,64]{1,0:T(4,128)S(1)} %get-tuple-element.238) | copy-start | bytes 2308 | tf_op jit(solution)/shard_map/while
  410.2 19.5 %copy-start.4 = (f32[3,64]{1,0:T(4,128)S(1)}, f32[3,64]{1,0:T(4,128)}, u32[]{:S(2)}) copy-start(f32[3,64]{1,0:T(4,128)} %copy-done.3) | copy-start | bytes 2308 | tf_op jit(solution)/shard_map/while
  410.2 19.5 %copy-start.11 = (s32[8]{0:T(128)S(1)}, s32[8]{0:T(128)}, u32[]{:S(2)}) copy-start(s32[8]{0:T(128)} %copy-done.10) | copy-start | bytes 100 | tf_op jit(solution)/shard_map/while
  430.5 10.2 %collective-permute-start.2 = (f32[1,3,64]{2,0,1:T(1,128)}, f32[1,3,64]{2,0,1:T(1,128)S(1)}, u32[]{:S(2)}, u32[]{:S(2)}) collective-permute-start(f32[1,3,64]{2,0,1:T(1,128)} %param.23), channel_id=1, source_target_pairs={{8,0},{16,8},{24,16},{9,1},{17,9},{25,17},{10,2},{18,10},{26,18},{... | collective-permute-start | bytes 2312 | tf_op jit(solution)/shard_map/ppermute | solution.py:19
  431.8 8.9 %collective-permute-start.3 = (f32[1,3,64]{2,0,1:T(1,128)}, f32[1,3,64]{2,0,1:T(1,128)S(1)}, u32[]{:S(2)}, u32[]{:S(2)}) collective-permute-start(f32[1,3,64]{2,0,1:T(1,128)} %param.23), channel_id=1, source_target_pairs={{0,8},{8,16},{16,24},{1,9},{9,17},{17,25},{2,10},{10,18},{18,26},{... | collective-permute-start | bytes 2312 | tf_op jit(solution)/shard_map/ppermute | solution.py:19
  471.5 6.0 %collective-permute-start.1 = (f32[1]{0:T(128)}, f32[1]{0:T(128)}, u32[]{:S(2)}, u32[]{:S(2)}) collective-permute-start(f32[1]{0:T(128)} %add.109), channel_id=1, source_target_pairs={{0,8},{8,16},{16,24},{1,9},{9,17},{17,25},{2,10},{10,18},{18,26},{... | collective-permute-start | bytes 20 | tf_op jit(solution)/shard_map/ppermute | solution.py:19
  476.2 5.4 %collective-permute-start = (f32[1]{0:T(128)}, f32[1]{0:T(128)}, u32[]{:S(2)}, u32[]{:S(2)}) collective-permute-start(f32[1]{0:T(128)} %add.109), channel_id=1, source_target_pairs={{8,0},{16,8},{24,16},{9,1},{17,9},{25,17},{10,2},{18,10},{26,18},{... | collective-permute-start | bytes 20 | tf_op jit(solution)/shard_map/ppermute | solution.py:19
  (27 other events, 98.7 us)
Sparse Core Ops, SparseCore 0:
  430.6 22.7 reduce-scatter.1
where the time goes:
time: 497 us; the launch traced here: 496 us
  other arithmetic  196 us (39%)
  matrix products  156 us (31%)
  local copies, waits for them, and re-layouts  74.8 us (15%)
  between operations  23.4 us (5%)
  blocking collectives  14.3 us (3%)
  waiting for transfers between devices  12.9 us (3%)
  starting transfers between devices  12.8 us (3%)
  loops' own time  6.05 us (1%)
    dot_general x8, matrix products, contract(): lax.dot_general(projector, stacked, (((1,), (1,)), ((), ())), preferred_e...  156 us
    another operation x9, other arithmetic  82.8 us
    cos x8, other arithmetic, projectors(): cosine = jnp.cos(phases)  69.1 us
    mul x16, local copies, waits for them, and re-layouts, projectors(): radial = species_mask[:, 0, :, None] * form_factor[0][None, :, :]  33.8 us
    concatenate x1, other arithmetic, stack_waves(): return jnp.concatenate(pieces, axis=0)  32.5 us
    unnamed x15, local copies, waits for them, and re-layouts  23.1 us
    psum x1, blocking collectives, per_device(): force_nl, energy_nl = lax.psum((force_full, energy_part), ('band', 'ga'))  14.3 us
    ppermute x4, starting transfers between devices, passed_along(): return lax.ppermute(array, axis, pairs)  12.8 us
  transfers between devices with their start and end apart: 5, of which 2 were waited for; matrix products, arithmetic and copies ran while one was open for 1% of the time, Pallas kernels for 0%

commit v1 on v0

--- a/solution.py
+++ b/solution.py
@@ -1,8 +1,10 @@
-import math
+import functools
 
 import jax
 import jax.numpy as jnp
 from jax import lax
+from jax.experimental import pallas as pl
+from jax.experimental.pallas import tpu as pltpu
 from jax.sharding import PartitionSpec as P
 
 ATOMS = 64
@@ -12,6 +14,97 @@
 
 spring_constant = 5.0
 
+
+S2=(7.07106765e-01, -2.94627488e-02, 3.68265567e-04, -2.18770204e-06, 7.15483753e-09)
+C2=(1.41421350e+00, -1.76776359e-01, 3.68257460e-03, -3.06124985e-05, 1.27899789e-07)
+P1=6.283203125; P2=-1.781782029e-05; IT=0.15915494309189535
+
+def cos_negsin(x):
+    k = jnp.round(x*IT)
+    r = (x - k*P1) - k*P2
+    y = r*r
+    s = S2[4]
+    for q in S2[3::-1]: s = s*y + q
+    s = s*r
+    c = C2[4]
+    for q in C2[3::-1]: c = c*y + q
+    return 1.0 - s*s, -(s*c)
+
+def body_trig(w_ref, ff_ref, g_ref, pos_ref, live_ref, cs, sn, fm, stk, off, gc, atoms, pmax, nspec, bands):
+    for j in range(gc//128):
+        sl = pl.ds(off+128*j, 128); dl = pl.ds(128*j,128); dl2 = pl.ds(gc+128*j,128)
+        g = [g_ref[c:c+1, sl] for c in range(3)]
+        for s in range(nspec):
+            fm[j, s] = ff_ref[s, :, sl]*live_ref[s]
+        for a in range(0, atoms, 8):
+            ph = pos_ref[0, a:a+8, :]*g[0]
+            ph = ph + pos_ref[1, a:a+8, :]*g[1]
+            ph = ph + pos_ref[2, a:a+8, :]*g[2]
+            co, ns = cos_negsin(ph)
+            cs[j, a:a+8, :] = co
+            sn[j, a:a+8, :] = ns
+        for n in range(0, bands, 16):
+            ub = w_ref[n:n+16, sl]; vb = w_ref[bands+n:bands+n+16, sl]
+            stk[n:n+16, dl] = ub; stk[n:n+16, dl2] = vb
+            u = ub.astype(jnp.float32); v = vb.astype(jnp.float32)
+            for c in range(3):
+                stk[(c+1)*bands+n:(c+1)*bands+n+16, dl] = (v*(-g[c])).astype(jnp.bfloat16)
+                stk[(c+1)*bands+n:(c+1)*bands+n+16, dl2] = (u*g[c]).astype(jnp.bfloat16)
+
+def body_mm(sp, acc, cs, sn, fm, stk, gc, atoms, pmax, rb):
+    for r0 in range(0, atoms*pmax, rb):
+        rows=[]
+        for a in range(r0//pmax, (r0+rb)//pmax, 16//pmax):
+            half=[]
+            for t in (cs, sn):
+                for j in range(gc//128):
+                    half.append(jnp.concatenate([fm[j, sp[b]]*t[j, pl.ds(b, pmax, stride=0), :] for b in range(a, a+16//pmax)],0).astype(jnp.bfloat16))
+            rows.append(jnp.concatenate(half,1))
+        P = jnp.concatenate(rows,0)
+        acc[r0:r0+rb, :] += lax.dot_general(P, stk[...], (((1,),(1,)),((),())), preferred_element_type=jnp.float32)
+
+def kern2(sp, w_ref, ff_ref, g_ref, pos_ref, live_ref, acc, csA, snA, fmA, csB, snB, fmB, sA, sB, *, gc, nsub, dims, rb):
+    i = pl.program_id(0)
+    atoms,pmax,nspec,bands = dims
+    @pl.when(i==0)
+    def _():
+        acc[...] = jnp.zeros_like(acc)
+        for r in (csB, snB, fmB, sB): r[...] = jnp.zeros_like(r)
+    gen = functools.partial(body_trig, w_ref, ff_ref, g_ref, pos_ref, live_ref)
+    def step(t, _):
+        base = pl.multiple_of(t*2*gc, 128)
+        gen(csA, snA, fmA, sA, base, gc, *dims)
+        body_mm(sp, acc, csB, snB, fmB, sB, gc, atoms, pmax, rb)
+        gen(csB, snB, fmB, sB, base+gc, gc, *dims)
+        body_mm(sp, acc, csA, snA, fmA, sA, gc, atoms, pmax, rb)
+        return 0
+    lax.fori_loop(0, nsub, step, 0)
+    @pl.when(i==pl.num_programs(0)-1)
+    def _():
+        body_mm(sp, acc, csB, snB, fmB, sB, gc, atoms, pmax, rb)
+        acc[...] = 2.0*acc[...]
+
+def contract(sp, w, ff, g, posb, live, gc=1024, blk=4096, rb=256):
+    nspec,pmax,G = ff.shape; atoms = posb.shape[1]; bands=w.shape[0]//2
+    rows=atoms*pmax
+    f32=jnp.float32; bf=jnp.bfloat16
+    blk=min(blk, G); gc=min(gc, blk//2)
+    return pl.pallas_call(
+        functools.partial(kern2, gc=gc, nsub=blk//(2*gc), dims=(atoms,pmax,nspec,bands), rb=rb),
+        grid=(G//blk,),
+        out_shape=jax.ShapeDtypeStruct((rows,4*bands), f32),
+        in_specs=[pl.BlockSpec(memory_space=pltpu.SMEM),
+            pl.BlockSpec((2*bands,blk), lambda i:(0,i)),
+            pl.BlockSpec((nspec,pmax,blk), lambda i:(0,0,i)),
+            pl.BlockSpec((3,blk), lambda i:(0,i)),
+            pl.BlockSpec((3,atoms,128), lambda i:(0,0,0)),
+            pl.BlockSpec((nspec,pmax,128), lambda i:(0,0,0))],
+        out_specs=pl.BlockSpec((rows,4*bands), lambda i:(0,0)),
+        scratch_shapes=[pltpu.VMEM((gc//128,atoms,128),f32),pltpu.VMEM((gc//128,atoms,128),f32),pltpu.VMEM((gc//128,nspec,pmax,128),f32)]*2
+          +[pltpu.VMEM((4*bands,2*gc),bf)]*2,
+        compiler_params=pltpu.CompilerParams(dimension_semantics=("arbitrary",), vmem_limit_bytes=48*2**20),
+        name="nl",
+    )(sp, w, ff, g, posb, live)
 
 def passed_along(array, axis, by):
     length = lax.axis_size(axis)
@@ -25,42 +118,6 @@
     species_mask = is_species[:, :, None] * is_live[None, :, :]
     strength = jnp.sum(species_mask * coupling[None, :, :], axis=1)
     return (species_mask, strength)
-
-
-def projectors(atom_pos, species_mask, form_factor, g_vectors):
-    phases = atom_pos[0][:, None] * g_vectors[0][None, :]
-    phases = phases + atom_pos[1][:, None] * g_vectors[1][None, :]
-    phases = phases + atom_pos[2][:, None] * g_vectors[2][None, :]
-    cosine = jnp.cos(phases)
-    sine_part = jnp.sin(phases)
-    radial = species_mask[:, 0, :, None] * form_factor[0][None, :, :]
-    for spec_num in range(1, SPECIES):
-        radial = radial + species_mask[:, spec_num, :, None] * form_factor[spec_num][None, :, :]
-    real_part = radial * cosine[:, None, :]
-    imag_part = -radial * sine_part[:, None, :]
-    joined = jnp.concatenate([real_part, imag_part], axis=-1).astype(jnp.bfloat16)
-    return joined.reshape(joined.shape[0] * joined.shape[1], joined.shape[2])
-
-
-def stack_waves(waves_here, g_vectors):
-    band_count = waves_here.shape[0]
-    real_part = waves_here[:, 0, :].astype(jnp.float32)
-    imag_part = waves_here[:, 1, :].astype(jnp.float32)
-    pieces = [waves_here.reshape(band_count, 2 * waves_here.shape[2])]
-    for axis_num in range(3):
-        direction = g_vectors[axis_num][None, :]
-        pieces.append(
-            jnp.concatenate([-direction * imag_part, direction * real_part], axis=-1).astype(
-                jnp.bfloat16
-            )
-        )
-    return jnp.concatenate(pieces, axis=0)
-
-
-def contract(projector, stacked):
-    return 2.0 * lax.dot_general(
-        projector, stacked, (((1,), (1,)), ((), ())), preferred_element_type=jnp.float32
-    )
 
 
 def nonlocal_terms(proj_sums, occupied, strength):
@@ -113,6 +170,41 @@
     return jnp.where(is_climb[:, None, None], climbing, regular)
 
 
+def swapped(array, axis, mask):
+    pairs = [(i, i ^ mask) for i in range(lax.axis_size(axis))]
+    return lax.ppermute(array, axis, pairs)
+
+
+def summed(array, axis):
+    size = lax.axis_size(axis)
+    if size & (size - 1):
+        return lax.psum(array, axis)
+    mask = 1
+    while mask < size:
+        array = array + swapped(array, axis, mask)
+        mask *= 2
+    return array
+
+
+def scattered_rows(rows, axis):
+    size = lax.axis_size(axis)
+    index = lax.axis_index(axis)
+    if size & (size - 1):
+        block = rows.shape[0] // size
+        return lax.psum_scatter(rows, axis, scatter_dimension=0, tiled=True), index * block
+    first = jnp.int32(0)
+    mask = 1
+    while mask < size:
+        half = rows.shape[0] // 2
+        bit = (index // mask) % 2
+        kept = lax.dynamic_slice_in_dim(rows, bit * half, half, 0)
+        sent = lax.dynamic_slice_in_dim(rows, (1 - bit) * half, half, 0)
+        rows = kept + swapped(sent, axis, mask)
+        first = first + bit * half
+        mask *= 2
+    return rows, first
+
+
 def per_device(
     wave_coeffs,
     occupation,
@@ -130,41 +222,37 @@
     tangent_kind,
 ):
     species_mask, strength = atom_tables(species, proj_count, coupling)
-    stacked = stack_waves(wave_coeffs[0], g_vectors)
-    atom_pos = positions[0]
-    occupied = occupation[0]
-    local_atoms = ATOMS // lax.axis_size("ga")
-    natoms = lax.axis_size("ga") * (local_atoms * PMAX) // PMAX
-    block_atoms = math.gcd(natoms, 8)
-    block_count = natoms // block_atoms
-
-    def one_block(block_num):
-        begin = block_num * block_atoms
-        pos_part = lax.dynamic_slice_in_dim(atom_pos, begin, block_atoms, 1)
-        mask_part = lax.dynamic_slice_in_dim(species_mask, begin, block_atoms, 0)
-        projector = projectors(pos_part, mask_part, form_factor, g_vectors)
-        return contract(projector, stacked)
-
-    blocks = lax.map(one_block, jnp.arange(block_count, dtype=jnp.int32))
-    proj_sums = lax.psum_scatter(
-        blocks.reshape(lax.axis_size("ga") * (local_atoms * PMAX), blocks.shape[2]),
-        "ga",
-        scatter_dimension=0,
-        tiled=True,
-    )
-    first_local = lax.axis_index("ga") * local_atoms
+    prev_pos = passed_along(positions, "image", 1)
+    next_pos = passed_along(positions, "image", -1)
+    bands = wave_coeffs.shape[1]
+    waves = wave_coeffs[0].transpose(1, 0, 2).reshape(2 * bands, wave_coeffs.shape[3])
+    is_live = (jnp.arange(PMAX)[None, :] < proj_count[:, None]).astype(jnp.float32)
+    sums = contract(
+        species,
+        waves,
+        form_factor,
+        g_vectors,
+        jnp.broadcast_to(positions[0][:, :, None], (3, ATOMS, 128)),
+        jnp.broadcast_to(is_live[:, :, None], (SPECIES, PMAX, 128)),
+    )
+    proj_sums, first_row = scattered_rows(sums, "ga")
+    first_local = first_row // PMAX
+    local_atoms = proj_sums.shape[0] // PMAX
     strength_part = lax.dynamic_slice_in_dim(strength, first_local, local_atoms, 0)
-    energy_part, force_part = nonlocal_terms(proj_sums, occupied, strength_part)
+    energy_part, force_part = nonlocal_terms(proj_sums, occupation[0], strength_part)
     force_full = lax.dynamic_update_slice_in_dim(
         jnp.zeros((3, ATOMS), jnp.float32), force_part, first_local, 1
     )
-    force_nl, energy_nl = lax.psum((force_full, energy_part), ("band", "ga"))
-    energy = energy_rest + energy_nl
-    force = force_rest + force_nl[None, :, :]
+    packed = jnp.concatenate(
+        [force_full, jnp.full((1, ATOMS), energy_part, jnp.float32)], axis=0
+    )
+    packed = summed(summed(packed, "band"), "ga")
+    energy = energy_rest + packed[3, :1]
+    force = force_rest + packed[None, :3, :]
     image_index = lax.axis_index("image")
     image_count = lax.axis_size("image")
-    prev_pos, prev_energy = passed_along((positions, energy), "image", 1)
-    next_pos, next_energy = passed_along((positions, energy), "image", -1)
+    prev_energy = passed_along(energy, "image", 1)
+    next_energy = passed_along(energy, "image", -1)
     at_start = image_index == 0
     at_end = image_index == image_count - 1
     prev_pos = jnp.where(at_start, end_positions[:1], prev_pos)

time: 497 us -> 130 us (0.26)
  other arithmetic: 196 us -> 5.47 us
  matrix products: 156 us -> 0 us
  Pallas kernels: 0 us -> 67.4 us
  local copies, waits for them, and re-layouts: 74.8 us -> 14.1 us
  blocking collectives: 14.3 us -> 0 us
  between operations: 23.4 us -> 10 us
  starting transfers between devices: 12.8 us -> 23.8 us
  loops' own time: 6.05 us -> 0 us
    dot_general x8 -> x0, matrix products: 156 us -> none  [contract(): lax.dot_general(projector, stacked, (((1,), (1,)), ((), ())), preferred_e...]
    another operation x9 -> x1, other arithmetic: 82.8 us -> 0.01 us  [nonlocal_terms(): return (energy_part, jnp.stack(forces, axis=0))]
    cos x8 -> x0, other arithmetic: 69.1 us -> none  [projectors(): cosine = jnp.cos(phases)]
    pallas_call x0 -> x1, Pallas kernels: none -> 67.4 us  [contract(): pl.pallas_call(functools.partial(kern2, gc=gc, nsub=blk // (2 * gc), dims...]
    mul x48 -> x0, local copies, waits for them, and re-layouts: 39.9 us -> none  [the longest x16 33.8 us: projectors(): radial = species_mask[:, 0, :, None] * form_factor[0][None, :, :]]
    concatenate x1 -> x0, other arithmetic: 32.5 us -> none  [stack_waves(): return jnp.concatenate(pieces, axis=0)]
    unnamed x15 -> x17, local copies, waits for them, and re-layouts: 23.1 us -> 0.04 us
    psum x1 -> x0, blocking collectives: 14.3 us -> none  [per_device(): force_nl, energy_nl = lax.psum((force_full, energy_part), ('band', 'ga'))]
  transfers between devices with their start and end apart: 5 -> 9, of which waited for: 2 -> 3; matrix products, arithmetic and copies ran while one was open for 1% -> 2% of each run, Pallas kernels for 0% -> 0%
where the time goes in v1:
time: 130 us; the launch traced here: 129 us
  Pallas kernels  67.4 us (52%)
  starting transfers between devices  23.8 us (18%)
  local copies, waits for them, and re-layouts  14.1 us (11%)
  between operations  10 us (8%)
  waiting for transfers between devices  8.63 us (7%)
  other arithmetic  5.47 us (4%)
    pallas_call x1, Pallas kernels, contract(): pl.pallas_call(functools.partial(kern2, gc=gc, nsub=blk // (2 * gc), dims...  67.4 us
    ppermute x4, starting transfers between devices, passed_along(): return lax.ppermute(array, axis, pairs)  12.7 us
    transpose x1, local copies, waits for them, and re-layouts, per_device(): wave_coeffs[0].transpose(1, 0, 2).reshape(2 * bands, wave_coeffs.shape[3])  11.3 us
    ppermute x5, starting transfers between devices, swapped(): return lax.ppermute(array, axis, pairs)  11.1 us
    ppermute x5, waiting for transfers between devices, swapped(): return lax.ppermute(array, axis, pairs)  5.84 us
    ppermute x4, waiting for transfers between devices, passed_along(): return lax.ppermute(array, axis, pairs)  2.79 us
  transfers between devices with their start and end apart: 9, of which 3 were waited for; matrix products, arithmetic and copies ran while one was open for 2% of the time, Pallas kernels for 0%

profile of v1, /device:TPU:0, one launch (start us, length us, event | category | flops | bytes accessed | tf_op | source)
XLA Modules:
  0.0 129.5 jit_solution(7868553792616786305)
XLA Ops:
  0.6 0.7 fusion.5
  1.4 11.3 %copy.18 = bf16[2,32,65536]{2,1,0:T(8,128)(2,1)} copy(bf16[2,32,65536]{2,0,1:T(2,128)(2,1)} %bitcast.29) | data formatting | bytes 16777216 | tf_op jit(solution)/shard_map/transpose | solution.py:228
  12.8 0.1 broadcast_in_dim.73.pos_ref
  12.9 67.4 %nl.1 = f32[512,128]{1,0:T(8,128)S(1)} custom-call(s32[64]{0:T(128)S(1)} %copy-done.1, bf16[64,65536]{1,0:T(8,128)(2,1)} %bitcast.28, f32[4,8,65536]{2,1,0:T(8,128)} %ff_ref.1, f32[3,65536]{1,0:T(4,128)S(1)} %copy-done, f32[3,64,128]{2,1,0:T(8,128)S(1)} %broadcast_in_dim.73.pos_ref, f32[4,8,128]{2,1,0:T(8,128)S(1)} %broadcast_in_dim.74.live_ref), custom_call_target="tpu_custom_call" | custom-call | tf_op jit(solution)/shard_map/nl/pallas_call | solution.py:92
  80.4 3.1 %collective-permute-start = (f32[256,128]{1,0:T(8,128)S(1)}, f32[256,128]{1,0:T(8,128)S(1)}, u32[]{:S(2)}, u32[]{:S(2)}) collective-permute-start(f32[256,128]{1,0:T(8,128)S(1)} %constant_dynamic-slice_fusion.1), channel_id=1, source_target_pairs={{0,1},{1,0},{2,3},{3,2},{4,5},{5,4},{6,7},{7,6},{8,9},{9,8},{10,11... | collective-permute-start | bytes 393224 | tf_op jit(solution)/shard_map/ppermute | solution.py:175
  83.5 3.5 %collective-permute-done = f32[256,128]{1,0:T(8,128)S(1)} collective-permute-done((f32[256,128]{1,0:T(8,128)S(1)}, f32[256,128]{1,0:T(8,128)S(1)}, u32[]{:S(2)}, u32[]{:S(2)}) %collective-permute-start) | collective-permute-done | bytes 131104 | tf_op jit(solution)/shard_map/ppermute | solution.py:175
  87.0 2.8 %collective-permute-start.1 = (f32[128,128]{1,0:T(8,128)S(1)}, f32[128,128]{1,0:T(8,128)S(1)}, u32[]{:S(2)}, u32[]{:S(2)}) collective-permute-start(f32[128,128]{1,0:T(8,128)S(1)} %constant_dynamic-slice_fusion), channel_id=1, source_target_pairs={{0,2},{1,3},{2,0},{3,1},{4,6},{5,7},{6,4},{7,5},{8,10},{9,11},{10,... | collective-permute-start | bytes 196616 | tf_op jit(solution)/shard_map/ppermute | solution.py:175
  89.9 2.3 %collective-permute-done.1 = f32[128,128]{1,0:T(8,128)S(1)} collective-permute-done((f32[128,128]{1,0:T(8,128)S(1)}, f32[128,128]{1,0:T(8,128)S(1)}, u32[]{:S(2)}, u32[]{:S(2)}) %collective-permute-start.1) | collective-permute-done | bytes 65568 | tf_op jit(solution)/shard_map/ppermute | solution.py:175
  92.3 0.2 fusion.3
  92.5 0.1 reshape.172
  92.7 0.1 reshape.173
  92.7 0.1 copy.20
  92.8 0.1 reshape.174
  92.9 0.1 copy.21
  93.1 0.1 copy.22
  93.2 0.7 multiply_reduce_fusion.1
  93.9 0.1 dynamic_update_slice.3
  94.0 0.7 concatenate.3
  94.8 1.3 collective-permute-start.7
  96.1 4.5 %collective-permute-start.8 = (f32[1,3,64]{2,0,1:T(1,128)S(1)}, f32[1,3,64]{2,0,1:T(1,128)S(1)}, u32[]{:S(2)}, u32[]{:S(2)}) collective-permute-start(f32[1,3,64]{2,0,1:T(1,128)S(1)} %copy-done.2), channel_id=1, source_target_pairs={{0,8},{8,16},{16,24},{1,9},{9,17},{17,25},{2,10},{10,18},{18,26},{... | collective-permute-start | bytes 2312 | tf_op jit(solution)/shard_map/ppermute | solution.py:112
  100.6 0.7 pad_add_fusion
  101.3 1.9 %collective-permute-start.3 = (f32[4,64]{1,0:T(4,128)S(1)}, f32[4,64]{1,0:T(4,128)S(1)}, u32[]{:S(2)}, u32[]{:S(2)}) collective-permute-start(f32[4,64]{1,0:T(4,128)S(1)} %pad_add_fusion), channel_id=1, source_target_pairs={{0,1},{1,0},{2,3},{3,2},{4,5},{5,4},{6,7},{7,6},{8,9},{9,8},{10,11... | collective-permute-start | bytes 3080 | tf_op jit(solution)/shard_map/ppermute | solution.py:175
  103.2 0.6 fusion.10
  105.8 3.2 %collective-permute-start.4 = (f32[4,64]{1,0:T(4,128)S(1)}, f32[4,64]{1,0:T(4,128)S(1)}, u32[]{:S(2)}, u32[]{:S(2)}) collective-permute-start(f32[4,64]{1,0:T(4,128)S(1)} %add.108), channel_id=1, source_target_pairs={{0,2},{1,3},{2,0},{3,1},{4,6},{5,7},{6,4},{7,5},{8,10},{9,11},{10,... | collective-permute-start | bytes 3080 | tf_op jit(solution)/shard_map/ppermute | solution.py:175
  109.0 0.6 multiply_reduce_fusion.8
  110.9 0.5 slice.36
  112.1 5.6 %collective-permute-start.6 = (f32[1]{0:T(128)}, f32[1]{0:T(128)}, u32[]{:S(2)}, u32[]{:S(2)}) collective-permute-start(f32[1]{0:T(128)} %add.111), channel_id=1, source_target_pairs={{0,8},{8,16},{16,24},{1,9},{9,17},{17,25},{2,10},{10,18},{18,26},{... | collective-permute-start | bytes 20 | tf_op jit(solution)/shard_map/ppermute | solution.py:112
  117.7 1.3 collective-permute-start.5
  120.3 2.8 %collective-permute-done.5 = f32[1]{0:T(128)} collective-permute-done((f32[1]{0:T(128)}, f32[1]{0:T(128)}, u32[]{:S(2)}, u32[]{:S(2)}) %collective-permute-start.5) | collective-permute-done | bytes 36 | tf_op jit(solution)/shard_map/ppermute | solution.py:112
  124.6 0.7 multiply_reduce_fusion.6
  126.0 0.6 multiply_reduce_fusion.5
  127.2 1.1 broadcast_select_fusion.5
  (39 shorter events, 0.5 us)
Async XLA Ops:
  1.4 11.3 %copy-start.2 = (f32[1,3,64]{2,0,1:T(1,128)S(1)}, f32[1,3,64]{2,0,1:T(1,128)}, u32[]{:S(2)}) copy-start(f32[1,3,64]{2,0,1:T(1,128)} %param.21) | copy-start | bytes 2308
  1.4 11.5 %copy-start = (f32[3,65536]{1,0:T(4,128)S(1)}, f32[3,65536]{1,0:T(4,128)}, u32[]{:S(2)}) copy-start(f32[3,65536]{1,0:T(4,128)} %g_ref.1) | copy-start | bytes 2359300
  1.4 11.5 %copy-start.1 = (s32[64]{0:T(128)S(1)}, s32[64]{0:T(128)}, u32[]{:S(2)}) copy-start(s32[64]{0:T(128)} %sp.1) | copy-start | bytes 772
  12.9 77.0 %copy-start.5 = (f32[4,8]{1,0:T(4,128)S(1)}, f32[4,8]{1,0:T(4,128)}, u32[]{:S(2)}) copy-start(f32[4,8]{1,0:T(4,128)} %param.20) | copy-start | bytes 388
  12.9 79.4 %copy-start.7 = (f32[1,32]{1,0:T(1,128)S(1)}, f32[1,32]{1,0:T(1,128)}, u32[]{:S(2)}) copy-start(f32[1,32]{1,0:T(1,128)} %param.15) | copy-start | bytes 388
  12.9 90.3 %copy-start.6 = (f32[2]{0:T(128)S(1)}, f32[2]{0:T(128)}, u32[]{:S(2)}) copy-start(f32[2]{0:T(128)} %param.25) | copy-start | bytes 28
  12.9 96.1 %copy-start.4 = (f32[2,3,64]{2,0,1:T(2,128)S(1)}, f32[2,3,64]{2,0,1:T(2,128)}, u32[]{:S(2)}) copy-start(f32[2,3,64]{2,0,1:T(2,128)} %param.24) | copy-start | bytes 4612
  12.9 113.1 %copy-start.3 = (f32[1,3,64]{2,0,1:T(1,128)S(1)}, f32[1,3,64]{2,0,1:T(1,128)}, u32[]{:S(2)}) copy-start(f32[1,3,64]{2,0,1:T(1,128)} %param.23) | copy-start | bytes 2308
  80.4 6.6 %collective-permute-start = (f32[256,128]{1,0:T(8,128)S(1)}, f32[256,128]{1,0:T(8,128)S(1)}, u32[]{:S(2)}, u32[]{:S(2)}) collective-permute-start(f32[256,128]{1,0:T(8,128)S(1)} %constant_dynamic-slice_fusion.1), channel_id=1, source_target_pairs={{0,1},{1,0},{2,3},{3,2},{4,5},{5,4},{6,7},{7,6},{8,9},{9,8},{10,11... | collective-permute-start | bytes 393224 | tf_op jit(solution)/shard_map/ppermute | solution.py:175
  87.0 5.2 %collective-permute-start.1 = (f32[128,128]{1,0:T(8,128)S(1)}, f32[128,128]{1,0:T(8,128)S(1)}, u32[]{:S(2)}, u32[]{:S(2)}) collective-permute-start(f32[128,128]{1,0:T(8,128)S(1)} %constant_dynamic-slice_fusion), channel_id=1, source_target_pairs={{0,2},{1,3},{2,0},{3,1},{4,6},{5,7},{6,4},{7,5},{8,10},{9,11},{10,... | collective-permute-start | bytes 196616 | tf_op jit(solution)/shard_map/ppermute | solution.py:175
  94.7 5.9 %collective-permute-start.2 = (f32[4,64]{1,0:T(4,128)S(1)}, f32[4,64]{1,0:T(4,128)S(1)}, u32[]{:S(2)}, u32[]{:S(2)}) collective-permute-start(f32[4,64]{1,0:T(4,128)S(1)} %concatenate.3), channel_id=1, source_target_pairs={{0,4},{4,0},{1,5},{5,1},{2,6},{6,2},{3,7},{7,3},{8,12},{12,8},{9,1... | collective-permute-start | bytes 3080 | tf_op jit(solution)/shard_map/ppermute | solution.py:175
  94.8 14.2 %collective-permute-start.7 = (f32[1,3,64]{2,0,1:T(1,128)S(1)}, f32[1,3,64]{2,0,1:T(1,128)S(1)}, u32[]{:S(2)}, u32[]{:S(2)}) collective-permute-start(f32[1,3,64]{2,0,1:T(1,128)S(1)} %copy-done.2), channel_id=1, source_target_pairs={{8,0},{16,8},{24,16},{9,1},{17,9},{25,17},{10,2},{18,10},{26,18},{... | collective-permute-start | bytes 2312 | tf_op jit(solution)/shard_map/ppermute | solution.py:112
  96.1 12.9 %collective-permute-start.8 = (f32[1,3,64]{2,0,1:T(1,128)S(1)}, f32[1,3,64]{2,0,1:T(1,128)S(1)}, u32[]{:S(2)}, u32[]{:S(2)}) collective-permute-start(f32[1,3,64]{2,0,1:T(1,128)S(1)} %copy-done.2), channel_id=1, source_target_pairs={{0,8},{8,16},{16,24},{1,9},{9,17},{17,25},{2,10},{10,18},{18,26},{... | collective-permute-start | bytes 2312 | tf_op jit(solution)/shard_map/ppermute | solution.py:112
  101.3 4.5 %collective-permute-start.3 = (f32[4,64]{1,0:T(4,128)S(1)}, f32[4,64]{1,0:T(4,128)S(1)}, u32[]{:S(2)}, u32[]{:S(2)}) collective-permute-start(f32[4,64]{1,0:T(4,128)S(1)} %pad_add_fusion), channel_id=1, source_target_pairs={{0,1},{1,0},{2,3},{3,2},{4,5},{5,4},{6,7},{7,6},{8,9},{9,8},{10,11... | collective-permute-start | bytes 3080 | tf_op jit(solution)/shard_map/ppermute | solution.py:175
  105.8 5.2 %collective-permute-start.4 = (f32[4,64]{1,0:T(4,128)S(1)}, f32[4,64]{1,0:T(4,128)S(1)}, u32[]{:S(2)}, u32[]{:S(2)}) collective-permute-start(f32[4,64]{1,0:T(4,128)S(1)} %add.108), channel_id=1, source_target_pairs={{0,2},{1,3},{2,0},{3,1},{4,6},{5,7},{6,4},{7,5},{8,10},{9,11},{10,... | collective-permute-start | bytes 3080 | tf_op jit(solution)/shard_map/ppermute | solution.py:175
  112.1 6.9 %collective-permute-start.6 = (f32[1]{0:T(128)}, f32[1]{0:T(128)}, u32[]{:S(2)}, u32[]{:S(2)}) collective-permute-start(f32[1]{0:T(128)} %add.111), channel_id=1, source_target_pairs={{0,8},{8,16},{16,24},{1,9},{9,17},{17,25},{2,10},{10,18},{18,26},{... | collective-permute-start | bytes 20 | tf_op jit(solution)/shard_map/ppermute | solution.py:112
  117.7 5.4 %collective-permute-start.5 = (f32[1]{0:T(128)}, f32[1]{0:T(128)}, u32[]{:S(2)}, u32[]{:S(2)}) collective-permute-start(f32[1]{0:T(128)} %add.111), channel_id=1, source_target_pairs={{8,0},{16,8},{24,16},{9,1},{17,9},{25,17},{10,2},{18,10},{26,18},{... | collective-permute-start | bytes 20 | tf_op jit(solution)/shard_map/ppermute | solution.py:112

commit v2 on v1

--- a/solution.py
+++ b/solution.py
@@ -13,6 +13,8 @@
 
 
 spring_constant = 5.0
+BLOCKS = 16
+CUTS = ((0, 4), (4, 4))
 
 
 S2=(7.07106765e-01, -2.94627488e-02, 3.68265567e-04, -2.18770204e-06, 7.15483753e-09)
@@ -30,81 +32,138 @@
     for q in C2[3::-1]: c = c*y + q
     return 1.0 - s*s, -(s*c)
 
-def body_trig(w_ref, ff_ref, g_ref, pos_ref, live_ref, cs, sn, fm, stk, off, gc, atoms, pmax, nspec, bands):
-    for j in range(gc//128):
-        sl = pl.ds(off+128*j, 128); dl = pl.ds(128*j,128); dl2 = pl.ds(gc+128*j,128)
-        g = [g_ref[c:c+1, sl] for c in range(3)]
-        for s in range(nspec):
-            fm[j, s] = ff_ref[s, :, sl]*live_ref[s]
+def make_chunk(waves, ff_ref, g_ref, pos_ref, live_ref, trig, stk, off):
+    cs, sn, fm = trig
+    chunk = stk.shape[1] // 2
+    atoms = pos_ref.shape[1]
+    for j in range(chunk // 128):
+        here = pl.ds(off + 128 * j, 128)
+        real = pl.ds(128 * j, 128)
+        imag = pl.ds(chunk + 128 * j, 128)
+        g = [g_ref[c : c + 1, here] for c in range(3)]
+        for s in range(ff_ref.shape[0]):
+            fm[j, s] = ff_ref[s, :, here] * live_ref[s]
         for a in range(0, atoms, 8):
-            ph = pos_ref[0, a:a+8, :]*g[0]
-            ph = ph + pos_ref[1, a:a+8, :]*g[1]
-            ph = ph + pos_ref[2, a:a+8, :]*g[2]
-            co, ns = cos_negsin(ph)
-            cs[j, a:a+8, :] = co
-            sn[j, a:a+8, :] = ns
-        for n in range(0, bands, 16):
-            ub = w_ref[n:n+16, sl]; vb = w_ref[bands+n:bands+n+16, sl]
-            stk[n:n+16, dl] = ub; stk[n:n+16, dl2] = vb
-            u = ub.astype(jnp.float32); v = vb.astype(jnp.float32)
-            for c in range(3):
-                stk[(c+1)*bands+n:(c+1)*bands+n+16, dl] = (v*(-g[c])).astype(jnp.bfloat16)
-                stk[(c+1)*bands+n:(c+1)*bands+n+16, dl2] = (u*g[c]).astype(jnp.bfloat16)
-
-def body_mm(sp, acc, cs, sn, fm, stk, gc, atoms, pmax, rb):
-    for r0 in range(0, atoms*pmax, rb):
-        rows=[]
-        for a in range(r0//pmax, (r0+rb)//pmax, 16//pmax):
-            half=[]
+            phase = pos_ref[0, a : a + 8, :] * g[0]
+            phase = phase + pos_ref[1, a : a + 8, :] * g[1]
+            phase = phase + pos_ref[2, a : a + 8, :] * g[2]
+            cosine, neg_sine = cos_negsin(phase)
+            cs[j, a : a + 8, :] = cosine
+            sn[j, a : a + 8, :] = neg_sine
+        row = 0
+        for w_ref in waves:
+            bands = w_ref.shape[0] // 2
+            for n in range(0, bands, 16):
+                u_in = w_ref[n : n + 16, here]
+                v_in = w_ref[bands + n : bands + n + 16, here]
+                stk[row + n : row + n + 16, real] = u_in.astype(jnp.bfloat16)
+                stk[row + n : row + n + 16, imag] = v_in.astype(jnp.bfloat16)
+                u = u_in.astype(jnp.float32)
+                v = v_in.astype(jnp.float32)
+                for c in range(3):
+                    at = row + (c + 1) * bands + n
+                    stk[at : at + 16, real] = (v * (-g[c])).astype(jnp.bfloat16)
+                    stk[at : at + 16, imag] = (u * g[c]).astype(jnp.bfloat16)
+            row += 4 * bands
+
+
+def multiply_chunk(sp, acc, trig, stk, rb):
+    cs, sn, fm = trig
+    lanes, _, pmax, _ = fm.shape
+    step = 16 // pmax
+    for r0 in range(0, acc.shape[0], rb):
+        rows = []
+        for a in range(r0 // pmax, (r0 + rb) // pmax, step):
+            parts = []
             for t in (cs, sn):
-                for j in range(gc//128):
-                    half.append(jnp.concatenate([fm[j, sp[b]]*t[j, pl.ds(b, pmax, stride=0), :] for b in range(a, a+16//pmax)],0).astype(jnp.bfloat16))
-            rows.append(jnp.concatenate(half,1))
-        P = jnp.concatenate(rows,0)
-        acc[r0:r0+rb, :] += lax.dot_general(P, stk[...], (((1,),(1,)),((),())), preferred_element_type=jnp.float32)
-
-def kern2(sp, w_ref, ff_ref, g_ref, pos_ref, live_ref, acc, csA, snA, fmA, csB, snB, fmB, sA, sB, *, gc, nsub, dims, rb):
+                for j in range(lanes):
+                    terms = [
+                        fm[j, sp[b]] * t[j, pl.ds(b, pmax, stride=0), :]
+                        for b in range(a, a + step)
+                    ]
+                    parts.append(jnp.concatenate(terms, 0).astype(jnp.bfloat16))
+            rows.append(jnp.concatenate(parts, 1))
+        acc[r0 : r0 + rb, :] += lax.dot_general(
+            jnp.concatenate(rows, 0),
+            stk[...],
+            (((1,), (1,)), ((), ())),
+            preferred_element_type=jnp.float32,
+        )
+
+
+def contract_kernel(*refs, parts, gc, rb):
+    sp, _, ff_ref, g_ref, pos_ref, live_ref = refs[:6]
+    waves = refs[6 : 6 + parts]
+    outs = refs[6 + parts : 6 + 2 * parts]
+    acc, csa, sna, fma, csb, snb, fmb, stka, stkb = refs[6 + 2 * parts :]
     i = pl.program_id(0)
-    atoms,pmax,nspec,bands = dims
-    @pl.when(i==0)
+    first = (csa, sna, fma)
+    second = (csb, snb, fmb)
+
+    @pl.when(i == 0)
     def _():
-        acc[...] = jnp.zeros_like(acc)
-        for r in (csB, snB, fmB, sB): r[...] = jnp.zeros_like(r)
-    gen = functools.partial(body_trig, w_ref, ff_ref, g_ref, pos_ref, live_ref)
-    def step(t, _):
-        base = pl.multiple_of(t*2*gc, 128)
-        gen(csA, snA, fmA, sA, base, gc, *dims)
-        body_mm(sp, acc, csB, snB, fmB, sB, gc, atoms, pmax, rb)
-        gen(csB, snB, fmB, sB, base+gc, gc, *dims)
-        body_mm(sp, acc, csA, snA, fmA, sA, gc, atoms, pmax, rb)
-        return 0
-    lax.fori_loop(0, nsub, step, 0)
-    @pl.when(i==pl.num_programs(0)-1)
+        for ref in (acc, csb, snb, fmb, stkb):
+            ref[...] = jnp.zeros_like(ref)
+
+    def step(t, carry):
+        base = pl.multiple_of(t * 2 * gc, 128)
+        make_chunk(waves, ff_ref, g_ref, pos_ref, live_ref, first, stka, base)
+        multiply_chunk(sp, acc, second, stkb, rb)
+        make_chunk(waves, ff_ref, g_ref, pos_ref, live_ref, second, stkb, base + gc)
+        multiply_chunk(sp, acc, first, stka, rb)
+        return carry
+
+    lax.fori_loop(0, g_ref.shape[1] // (2 * gc), step, 0)
+
+    @pl.when(i == pl.num_programs(0) - 1)
     def _():
-        body_mm(sp, acc, csB, snB, fmB, sB, gc, atoms, pmax, rb)
-        acc[...] = 2.0*acc[...]
-
-def contract(sp, w, ff, g, posb, live, gc=1024, blk=4096, rb=256):
-    nspec,pmax,G = ff.shape; atoms = posb.shape[1]; bands=w.shape[0]//2
-    rows=atoms*pmax
-    f32=jnp.float32; bf=jnp.bfloat16
-    blk=min(blk, G); gc=min(gc, blk//2)
+        multiply_chunk(sp, acc, second, stkb, rb)
+        cols = outs[0].shape[1]
+        for k in range(parts):
+            outs[k][...] = 2.0 * acc[:, k * cols : (k + 1) * cols]
+
+
+def contract(sp, start, waves, ff, g, posb, live, gc=1024, blk=4096, rb=256):
+    nspec, pmax, _ = ff.shape
+    atoms = posb.shape[1]
+    parts = len(waves)
+    length = waves[0].shape[1]
+    rows, cols = atoms * pmax, 2 * waves[0].shape[0]
+    trig = [
+        pltpu.VMEM((gc // 128, atoms, 128), jnp.float32),
+        pltpu.VMEM((gc // 128, atoms, 128), jnp.float32),
+        pltpu.VMEM((gc // 128, nspec, pmax, 128), jnp.float32),
+    ]
+    stk = pltpu.VMEM((parts * cols, 2 * gc), jnp.bfloat16)
     return pl.pallas_call(
-        functools.partial(kern2, gc=gc, nsub=blk//(2*gc), dims=(atoms,pmax,nspec,bands), rb=rb),
-        grid=(G//blk,),
-        out_shape=jax.ShapeDtypeStruct((rows,4*bands), f32),
-        in_specs=[pl.BlockSpec(memory_space=pltpu.SMEM),
-            pl.BlockSpec((2*bands,blk), lambda i:(0,i)),
-            pl.BlockSpec((nspec,pmax,blk), lambda i:(0,0,i)),
-            pl.BlockSpec((3,blk), lambda i:(0,i)),
-            pl.BlockSpec((3,atoms,128), lambda i:(0,0,0)),
-            pl.BlockSpec((nspec,pmax,128), lambda i:(0,0,0))],
-        out_specs=pl.BlockSpec((rows,4*bands), lambda i:(0,0)),
-        scratch_shapes=[pltpu.VMEM((gc//128,atoms,128),f32),pltpu.VMEM((gc//128,atoms,128),f32),pltpu.VMEM((gc//128,nspec,pmax,128),f32)]*2
-          +[pltpu.VMEM((4*bands,2*gc),bf)]*2,
-        compiler_params=pltpu.CompilerParams(dimension_semantics=("arbitrary",), vmem_limit_bytes=48*2**20),
-        name="nl",
-    )(sp, w, ff, g, posb, live)
+        functools.partial(contract_kernel, parts=parts, gc=gc, rb=rb),
+        grid_spec=pltpu.PrefetchScalarGridSpec(
+            num_scalar_prefetch=2,
+            grid=(length // blk,),
+            in_specs=[
+                pl.BlockSpec((nspec, pmax, blk), lambda i, sp, st: (0, 0, st[0] + i)),
+                pl.BlockSpec((3, blk), lambda i, sp, st: (0, st[0] + i)),
+                pl.BlockSpec((3, atoms, 128), lambda i, sp, st: (0, 0, 0)),
+                pl.BlockSpec((nspec, pmax, 128), lambda i, sp, st: (0, 0, 0)),
+            ]
+            + [pl.BlockSpec((w.shape[0], blk), lambda i, sp, st: (0, i)) for w in waves],
+            out_specs=[pl.BlockSpec((rows, cols), lambda i, sp, st: (0, 0))] * parts,
+            scratch_shapes=[pltpu.VMEM((rows, parts * cols), jnp.float32)]
+            + trig * 2
+            + [stk] * 2,
+        ),
+        out_shape=[jax.ShapeDtypeStruct((rows, cols), jnp.float32)] * parts,
+        compiler_params=pltpu.CompilerParams(
+            dimension_semantics=("arbitrary",), vmem_limit_bytes=48 * 2**20
+        ),
+        cost_estimate=pl.CostEstimate(
+            flops=4 * rows * parts * cols * length,
+            bytes_accessed=8 * length * (nspec * pmax + 3),
+            transcendentals=0,
+        ),
+        name="contract",
+    )(sp, start, ff, g, posb, live, *waves)
+
 
 def passed_along(array, axis, by):
     length = lax.axis_size(axis)
@@ -222,19 +281,34 @@
     tangent_kind,
 ):
     species_mask, strength = atom_tables(species, proj_count, coupling)
-    prev_pos = passed_along(positions, "image", 1)
-    next_pos = passed_along(positions, "image", -1)
     bands = wave_coeffs.shape[1]
-    waves = wave_coeffs[0].transpose(1, 0, 2).reshape(2 * bands, wave_coeffs.shape[3])
+    length = wave_coeffs.shape[3]
     is_live = (jnp.arange(PMAX)[None, :] < proj_count[:, None]).astype(jnp.float32)
-    sums = contract(
-        species,
-        waves,
-        form_factor,
-        g_vectors,
-        jnp.broadcast_to(positions[0][:, :, None], (3, ATOMS, 128)),
-        jnp.broadcast_to(is_live[:, :, None], (SPECIES, PMAX, 128)),
-    )
+    posb = jnp.broadcast_to(positions[0][:, :, None], (3, ATOMS, 128))
+    live = jnp.broadcast_to(is_live[:, :, None], (SPECIES, PMAX, 128))
+    blk = length // BLOCKS
+    half = BLOCKS // 2
+    core = lax.axis_index("band") % 2
+
+    def rows_of(first, count):
+        part = lax.dynamic_slice_in_dim(wave_coeffs[0], first * blk, count * blk, 2)
+        return part.transpose(1, 0, 2).reshape(2 * bands, count * blk)
+
+    chunks = []
+    for at, count in CUTS:
+        given = rows_of((1 - core) * half + at, count).astype(jnp.float32)
+        chunks.append((core * half + at, count, swapped(given, "band", 1)))
+    mine = 0.0
+    other = 0.0
+    for first, count, taken in chunks:
+        kept = rows_of(first, count)
+        start = first.astype(jnp.int32)[None]
+        own_sums, other_sums = contract(
+            species, start, [kept, taken], form_factor, g_vectors, posb, live, blk=blk
+        )
+        mine = mine + own_sums
+        other = other + other_sums
+    sums = mine + swapped(other, "band", 1)
     proj_sums, first_row = scattered_rows(sums, "ga")
     first_local = first_row // PMAX
     local_atoms = proj_sums.shape[0] // PMAX
@@ -251,8 +325,11 @@
     force = force_rest + packed[None, :3, :]
     image_index = lax.axis_index("image")
     image_count = lax.axis_size("image")
-    prev_energy = passed_along(energy, "image", 1)
-    next_energy = passed_along(energy, "image", -1)
+    sent = jnp.concatenate([positions[0], jnp.broadcast_to(energy[:, None], (1, ATOMS))], axis=0)
+    before = passed_along(sent, "image", 1)
+    after = passed_along(sent, "image", -1)
+    prev_pos, prev_energy = before[None, :3, :], before[3, :1]
+    next_pos, next_energy = after[None, :3, :], after[3, :1]
     at_start = image_index == 0
     at_end = image_index == image_count - 1
     prev_pos = jnp.where(at_start, end_positions[:1], prev_pos)

time: 130 us -> 112 us (0.86)
  Pallas kernels: 67.4 us -> 43.9 us
  other arithmetic: 5.47 us -> 14 us
  starting transfers between devices: 23.8 us -> 16.2 us
  waiting for transfers between devices: 8.63 us -> 14.5 us
    pallas_call x1 -> x2, Pallas kernels: 67.4 us -> 43.9 us  [contract(): pl.pallas_call(functools.partial(contract_kernel, parts=parts, gc=gc, rb=...]
    transpose x1 -> x0, local copies, waits for them, and re-layouts: 11.3 us -> none  [per_device(): wave_coeffs[0].transpose(1, 0, 2).reshape(2 * bands, wave_coeffs.shape[3])]
    convert_element_type x0 -> x1, other arithmetic: none -> 8.51 us  [per_device(): given = rows_of((1 - core) * half + at, count).astype(jnp.float32)]
    ppermute x4 -> x2, starting transfers between devices: 12.7 us -> 4.68 us  [passed_along(): return lax.ppermute(array, axis, pairs)]
    ppermute x5 -> x8, waiting for transfers between devices: 5.84 us -> 13.4 us  [swapped(): return lax.ppermute(array, axis, pairs)]
    convert_element_type x0 -> x2, local copies, waits for them, and re-layouts: none -> 4.86 us  [per_device(): given = rows_of((1 - core) * half + at, count).astype(jnp.float32)]
    unnamed x17 -> x23, local copies, waits for them, and re-layouts: 0.04 us -> 4.25 us
    ppermute x4 -> x2, waiting for transfers between devices: 2.79 us -> 1.14 us  [passed_along(): return lax.ppermute(array, axis, pairs)]
  transfers between devices with their start and end apart: 9 -> 10, of which waited for: 3 -> 8; matrix products, arithmetic and copies ran while one was open for 2% -> 6% of each run, Pallas kernels for 0% -> 20%
where the time goes in v2:
time: 112 us
  Pallas kernels  43.9 us (39%)
  starting transfers between devices  16.2 us (14%)
  waiting for transfers between devices  14.5 us (13%)
  other arithmetic  14 us (12%)
  local copies, waits for them, and re-layouts  12.9 us (12%)
  between operations  10.1 us (9%)
    pallas_call x2, Pallas kernels, contract(): pl.pallas_call(functools.partial(contract_kernel, parts=parts, gc=gc, rb=...  43.9 us
    ppermute x8, waiting for transfers between devices, swapped(): return lax.ppermute(array, axis, pairs)  13.4 us
    ppermute x8, starting transfers between devices, swapped(): return lax.ppermute(array, axis, pairs)  11.5 us
    convert_element_type x1, other arithmetic, per_device(): given = rows_of((1 - core) * half + at, count).astype(jnp.float32)  8.51 us
    convert_element_type x2, local copies, waits for them, and re-layouts, per_device(): given = rows_of((1 - core) * half + at, count).astype(jnp.float32)  4.86 us
    ppermute x2, starting transfers between devices, passed_along(): return lax.ppermute(array, axis, pairs)  4.68 us
    unnamed x23, local copies, waits for them, and re-layouts  4.25 us
  transfers between devices with their start and end apart: 10, of which 8 were waited for; matrix products, arithmetic and copies ran while one was open for 6% of the time, Pallas kernels for 20%

profile of v2, /device:TPU:0, one launch (start us, length us, event | category | flops | bytes accessed | tf_op | source)
XLA Modules:
  0.0 111.7 jit_solution(5246447578674381615)
XLA Ops:
  0.7 8.5 %convert_bitcast_fusion = (f32[2,32,16384]{2,0,1:T(2,128)S(1)}, bf16[1,32,2,16384]{3,2,1,0:T(2,128)(2,1)S(1)}, bf16[1,32,2,16384]{3,2,1,0:T(2,128)(2,1)S(1)}, f32[2,32,16384]{2,0,1:T(2,128)S(1)}) fusion(bf16[1,32,2,65536]{3,2,1,0:T(2,128)(2,1)} %param.14, s32[]{:T(128)S(6)} %select_n.108, s32[]{:T(128)S(6)} %select_n.105, s32[]{:T(128)S(6)} %select_n.107, ...), kind=kLoop, calls=%fused_computation | loop fusion | flops 2097152 | bytes 20971536 | tf_op jit(solution)/shard_map/convert_element_type | solution.py:299
  9.2 2.4 %copy.29 = f32[2,32,16384]{2,1,0:T(8,128)S(1)} copy(f32[2,32,16384]{2,0,1:T(2,128)S(1)} %get-tuple-element.24) | data formatting | bytes 8388608 | tf_op jit(solution)/shard_map/convert_element_type | solution.py:299
  11.6 0.6 collective-permute-start.1
  12.2 2.4 %copy.27 = f32[2,32,16384]{2,1,0:T(8,128)S(1)} copy(f32[2,32,16384]{2,0,1:T(2,128)S(1)} %get-tuple-element.27) | data formatting | bytes 8388608 | tf_op jit(solution)/shard_map/convert_element_type | solution.py:299
  14.7 1.2 %copy.38 = bf16[1,32,2,16384]{3,1,2,0:T(8,128)(2,1)S(1)} copy(bf16[1,32,2,16384]{3,2,1,0:T(2,128)(2,1)S(1)} %get-tuple-element.26) | data formatting | bytes 4194304
  15.9 1.2 %copy.37 = bf16[1,32,2,16384]{3,1,2,0:T(8,128)(2,1)S(1)} copy(bf16[1,32,2,16384]{3,2,1,0:T(2,128)(2,1)S(1)} %get-tuple-element.25) | data formatting | bytes 4194304
  17.2 1.8 %collective-permute-done.1.refs_7_ = f32[64,16384]{1,0:T(8,128)S(1)} collective-permute-done((f32[64,16384]{1,0:T(8,128)S(1)}, f32[64,16384]{1,0:T(8,128)S(1)}, u32[]{:S(2)}, u32[]{:S(2)}) %collective-permute-start.1) | collective-permute-done | bytes 4194336 | tf_op jit(solution)/shard_map/ppermute | solution.py:234
  19.1 1.9 %copy-done.9 = f32[64,16384]{1,0:T(8,128)} copy-done((f32[64,16384]{1,0:T(8,128)}, f32[64,16384]{1,0:T(8,128)S(1)}, u32[]{:S(2)}) %copy-start.9) | copy-done | bytes 4194328
  21.0 22.0 %contract.3 = (f32[512,128]{1,0:T(8,128)S(1)}, f32[512,128]{1,0:T(8,128)S(1)}) custom-call(s32[64]{0:T(128)S(1)} %copy-done, s32[1]{0:T(128)} %bitcast.9.refs_1_, f32[4,8,65536]{2,1,0:T(8,128)} %refs_2_.3, f32[3,65536]{1,0:T(4,128)S(1)} %copy-done.1, f32[3,64,128]{2,1,0:T(8,128)S(1)} %broadcast_in_dim.92.refs_4_, f32[4,8,128]{2,1,0:T(8,128)S(1)} %broadcast_in_dim.93.refs_5_, ...), custom_call_target="tpu_custom_call" | custom-call | flops 8589934592 | bytes 4587520 | tf_op jit(solution)/shard_map/contract/pallas_call | solution.py:138
  43.1 21.9 %contract.2 = (f32[512,128]{1,0:T(8,128)S(1)}, f32[512,128]{1,0:T(8,128)S(1)}) custom-call(s32[64]{0:T(128)S(1)} %copy-done, s32[1]{0:T(128)} %bitcast.2.refs_1_, f32[4,8,65536]{2,1,0:T(8,128)} %refs_2_.3, f32[3,65536]{1,0:T(4,128)S(1)} %copy-done.1, f32[3,64,128]{2,1,0:T(8,128)S(1)} %broadcast_in_dim.92.refs_4_, f32[4,8,128]{2,1,0:T(8,128)S(1)} %broadcast_in_dim.93.refs_5_, ...), custom_call_target="tpu_custom_call" | custom-call | flops 8589934592 | bytes 4587520 | tf_op jit(solution)/shard_map/contract/pallas_call | solution.py:138
  65.5 1.2 %collective-permute-done.2 = f32[512,128]{1,0:T(8,128)S(1)} collective-permute-done((f32[512,128]{1,0:T(8,128)S(1)}, f32[512,128]{1,0:T(8,128)S(1)}, u32[]{:S(2)}, u32[]{:S(2)}) %collective-permute-start.2) | collective-permute-done | bytes 262176 | tf_op jit(solution)/shard_map/ppermute | solution.py:234
  66.7 3.0 %collective-permute-start.3 = (f32[256,128]{1,0:T(8,128)S(1)}, f32[256,128]{1,0:T(8,128)S(1)}, u32[]{:S(2)}, u32[]{:S(2)}) collective-permute-start(f32[256,128]{1,0:T(8,128)S(1)} %constant_dynamic-slice_fusion.1), channel_id=1, source_target_pairs={{0,1},{1,0},{2,3},{3,2},{4,5},{5,4},{6,7},{7,6},{8,9},{9,8},{10,11... | collective-permute-start | bytes 393224 | tf_op jit(solution)/shard_map/ppermute | solution.py:234
  69.7 3.8 %collective-permute-done.3 = f32[256,128]{1,0:T(8,128)S(1)} collective-permute-done((f32[256,128]{1,0:T(8,128)S(1)}, f32[256,128]{1,0:T(8,128)S(1)}, u32[]{:S(2)}, u32[]{:S(2)}) %collective-permute-start.3) | collective-permute-done | bytes 131104 | tf_op jit(solution)/shard_map/ppermute | solution.py:234
  73.5 2.8 %collective-permute-start.4 = (f32[128,128]{1,0:T(8,128)S(1)}, f32[128,128]{1,0:T(8,128)S(1)}, u32[]{:S(2)}, u32[]{:S(2)}) collective-permute-start(f32[128,128]{1,0:T(8,128)S(1)} %constant_dynamic-slice_fusion), channel_id=1, source_target_pairs={{0,2},{1,3},{2,0},{3,1},{4,6},{5,7},{6,4},{7,5},{8,10},{9,11},{10,... | collective-permute-start | bytes 196616 | tf_op jit(solution)/shard_map/ppermute | solution.py:234
  76.4 2.5 %collective-permute-done.4 = f32[128,128]{1,0:T(8,128)S(1)} collective-permute-done((f32[128,128]{1,0:T(8,128)S(1)}, f32[128,128]{1,0:T(8,128)S(1)}, u32[]{:S(2)}, u32[]{:S(2)}) %collective-permute-start.4) | collective-permute-done | bytes 65568 | tf_op jit(solution)/shard_map/ppermute | solution.py:234
  79.9 0.7 multiply_reduce_fusion.1
  80.7 0.7 concatenate.6
  81.5 1.1 %collective-permute-done.5 = f32[4,64]{1,0:T(4,128)S(1)} collective-permute-done((f32[4,64]{1,0:T(4,128)S(1)}, f32[4,64]{1,0:T(4,128)S(1)}, u32[]{:S(2)}, u32[]{:S(2)}) %collective-permute-start.5) | collective-permute-done | bytes 1056 | tf_op jit(solution)/shard_map/ppermute | solution.py:234
  82.6 0.7 pad_add_fusion
  83.3 1.7 %collective-permute-start.6 = (f32[4,64]{1,0:T(4,128)S(1)}, f32[4,64]{1,0:T(4,128)S(1)}, u32[]{:S(2)}, u32[]{:S(2)}) collective-permute-start(f32[4,64]{1,0:T(4,128)S(1)} %pad_add_fusion), channel_id=1, source_target_pairs={{0,1},{1,0},{2,3},{3,2},{4,5},{5,4},{6,7},{7,6},{8,9},{9,8},{10,11... | collective-permute-start | bytes 3080 | tf_op jit(solution)/shard_map/ppermute | solution.py:234
  85.0 1.9 %collective-permute-done.6 = f32[4,64]{1,0:T(4,128)S(1)} collective-permute-done((f32[4,64]{1,0:T(4,128)S(1)}, f32[4,64]{1,0:T(4,128)S(1)}, u32[]{:S(2)}, u32[]{:S(2)}) %collective-permute-start.6) | collective-permute-done | bytes 1056 | tf_op jit(solution)/shard_map/ppermute | solution.py:234
  86.9 2.8 %collective-permute-start.7 = (f32[4,64]{1,0:T(4,128)S(1)}, f32[4,64]{1,0:T(4,128)S(1)}, u32[]{:S(2)}, u32[]{:S(2)}) collective-permute-start(f32[4,64]{1,0:T(4,128)S(1)} %add.150), channel_id=1, source_target_pairs={{0,2},{1,3},{2,0},{3,1},{4,6},{5,7},{6,4},{7,5},{8,10},{9,11},{10,... | collective-permute-start | bytes 3080 | tf_op jit(solution)/shard_map/ppermute | solution.py:234
  90.4 1.0 collective-permute-done.7
  92.6 3.4 %collective-permute-start.9 = (f32[4,64]{1,0:T(4,128)S(1)}, f32[4,64]{1,0:T(4,128)S(1)}, u32[]{:S(2)}, u32[]{:S(2)}) collective-permute-start(f32[4,64]{1,0:T(4,128)S(1)} %concatenate.7), channel_id=1, source_target_pairs={{0,8},{8,16},{16,24},{1,9},{9,17},{17,25},{2,10},{10,18},{18,26},{... | collective-permute-start | bytes 3080 | tf_op jit(solution)/shard_map/ppermute | solution.py:171
  96.0 0.7 fusion.8
  96.7 1.3 %collective-permute-start.8 = (f32[4,64]{1,0:T(4,128)S(1)}, f32[4,64]{1,0:T(4,128)S(1)}, u32[]{:S(2)}, u32[]{:S(2)}) collective-permute-start(f32[4,64]{1,0:T(4,128)S(1)} %concatenate.7), channel_id=1, source_target_pairs={{8,0},{16,8},{24,16},{9,1},{17,9},{25,17},{10,2},{18,10},{26,18},{... | collective-permute-start | bytes 3080 | tf_op jit(solution)/shard_map/ppermute | solution.py:171
  101.0 1.1 %collective-permute-done.8 = f32[4,64]{1,0:T(4,128)S(1)} collective-permute-done((f32[4,64]{1,0:T(4,128)S(1)}, f32[4,64]{1,0:T(4,128)S(1)}, u32[]{:S(2)}, u32[]{:S(2)}) %collective-permute-start.8) | collective-permute-done | bytes 1056 | tf_op jit(solution)/shard_map/ppermute | solution.py:171
  104.1 0.6 multiply_reduce_fusion.7
  105.5 0.6 multiply_reduce_fusion.8
  106.8 0.7 multiply_reduce_fusion.6
  108.3 0.6 multiply_reduce_fusion.5
  109.4 1.1 %broadcast_select_fusion.4 = f32[1,3,64]{2,0,1:T(1,128)} fusion(pred[]{:T(512)} %bitcast.1, f32[1,3,64]{2,0,1:T(1,128)S(1)} %get-tuple-element.19, f32[]{:T(128)} %bitcast.34, f32[]{:T(128)} %get-tuple-element.18, f32[]{:T(128)S(6)} %mul.251, f32[1,3,64]{2,0,1:T(1,128)S(1)} %copy-done.3, f32[3,64]{1,0:T(4,128)S(1)} %bitcast.61), kind=kLoop, calls=%fused_computation.22 | loop fusion | flops 1536 | bytes 3085 | tf_op jit(solution)/shard_map/jit(_where)/select_n | solution.py:229
  (57 shorter events, 3.7 us)
Async XLA Ops:
  11.6 7.3 %collective-permute-start.1 = (f32[64,16384]{1,0:T(8,128)S(1)}, f32[64,16384]{1,0:T(8,128)S(1)}, u32[]{:S(2)}, u32[]{:S(2)}) collective-permute-start(f32[64,16384]{1,0:T(8,128)S(1)} %bitcast.57), channel_id=1, source_target_pairs={{0,4},{4,0},{1,5},{5,1},{2,6},{6,2},{3,7},{7,3},{8,12},{12,8},{9,1... | collective-permute-start | bytes 12582920 | tf_op jit(solution)/shard_map/ppermute | solution.py:234
  14.6 1.3 %copy-start.2 = (f32[1,3,64]{2,0,1:T(1,128)S(1)}, f32[1,3,64]{2,0,1:T(1,128)}, u32[]{:S(2)}) copy-start(f32[1,3,64]{2,0,1:T(1,128)} %param.21) | copy-start | bytes 2308
  14.6 28.4 %collective-permute-start = (f32[64,16384]{1,0:T(8,128)S(1)}, f32[64,16384]{1,0:T(8,128)}, u32[]{:S(2)}, u32[]{:S(2)}) collective-permute-start(f32[64,16384]{1,0:T(8,128)S(1)} %bitcast.56), channel_id=1, source_target_pairs={{0,4},{4,0},{1,5},{5,1},{2,6},{6,2},{3,7},{7,3},{8,12},{12,8},{9,1... | collective-permute-start | bytes 12582920 | tf_op jit(solution)/shard_map/ppermute | solution.py:234
  14.7 2.4 %copy-start.8 = (s32[4]{0:T(128)S(1)}, s32[4]{0:T(128)}, u32[]{:S(2)}) copy-start(s32[4]{0:T(128)} %param.19) | copy-start | bytes 52
  14.7 6.3 %copy-start = (s32[64]{0:T(128)S(1)}, s32[64]{0:T(128)}, u32[]{:S(2)}) copy-start(s32[64]{0:T(128)} %refs_0_.3) | copy-start | bytes 772
  14.7 6.3 %copy-start.1 = (f32[3,65536]{1,0:T(4,128)S(1)}, f32[3,65536]{1,0:T(4,128)}, u32[]{:S(2)}) copy-start(f32[3,65536]{1,0:T(4,128)} %refs_3_.3) | copy-start | bytes 2359300
  19.0 2.0 %copy-start.9 = (f32[64,16384]{1,0:T(8,128)}, f32[64,16384]{1,0:T(8,128)S(1)}, u32[]{:S(2)}) copy-start(f32[64,16384]{1,0:T(8,128)S(1)} %collective-permute-done.1.refs_7_) | copy-start | bytes 12582916
  43.1 33.3 %copy-start.5 = (f32[4,8]{1,0:T(4,128)S(1)}, f32[4,8]{1,0:T(4,128)}, u32[]{:S(2)}) copy-start(f32[4,8]{1,0:T(4,128)} %param.20) | copy-start | bytes 388
  43.1 35.9 %copy-start.7 = (f32[1,32]{1,0:T(1,128)S(1)}, f32[1,32]{1,0:T(1,128)}, u32[]{:S(2)}) copy-start(f32[1,32]{1,0:T(1,128)} %param.15) | copy-start | bytes 388
  43.1 52.9 %copy-start.6 = (f32[2]{0:T(128)S(1)}, f32[2]{0:T(128)}, u32[]{:S(2)}) copy-start(f32[2]{0:T(128)} %param.25) | copy-start | bytes 28
  43.1 61.0 %copy-start.4 = (f32[2,3,64]{2,0,1:T(2,128)S(1)}, f32[2,3,64]{2,0,1:T(2,128)}, u32[]{:S(2)}) copy-start(f32[2,3,64]{2,0,1:T(2,128)} %param.24) | copy-start | bytes 4612
  43.1 65.2 %copy-start.3 = (f32[1,3,64]{2,0,1:T(1,128)S(1)}, f32[1,3,64]{2,0,1:T(1,128)}, u32[]{:S(2)}) copy-start(f32[1,3,64]{2,0,1:T(1,128)} %param.23) | copy-start | bytes 2308
  65.0 1.6 %collective-permute-start.2 = (f32[512,128]{1,0:T(8,128)S(1)}, f32[512,128]{1,0:T(8,128)S(1)}, u32[]{:S(2)}, u32[]{:S(2)}) collective-permute-start(f32[512,128]{1,0:T(8,128)S(1)} %add.141), channel_id=1, source_target_pairs={{0,4},{4,0},{1,5},{5,1},{2,6},{6,2},{3,7},{7,3},{8,12},{12,8},{9,1... | collective-permute-start | bytes 786440 | tf_op jit(solution)/shard_map/ppermute | solution.py:234
  66.7 6.8 %collective-permute-start.3 = (f32[256,128]{1,0:T(8,128)S(1)}, f32[256,128]{1,0:T(8,128)S(1)}, u32[]{:S(2)}, u32[]{:S(2)}) collective-permute-start(f32[256,128]{1,0:T(8,128)S(1)} %constant_dynamic-slice_fusion.1), channel_id=1, source_target_pairs={{0,1},{1,0},{2,3},{3,2},{4,5},{5,4},{6,7},{7,6},{8,9},{9,8},{10,11... | collective-permute-start | bytes 393224 | tf_op jit(solution)/shard_map/ppermute | solution.py:234
  73.5 5.4 %collective-permute-start.4 = (f32[128,128]{1,0:T(8,128)S(1)}, f32[128,128]{1,0:T(8,128)S(1)}, u32[]{:S(2)}, u32[]{:S(2)}) collective-permute-start(f32[128,128]{1,0:T(8,128)S(1)} %constant_dynamic-slice_fusion), channel_id=1, source_target_pairs={{0,2},{1,3},{2,0},{3,1},{4,6},{5,7},{6,4},{7,5},{8,10},{9,11},{10,... | collective-permute-start | bytes 196616 | tf_op jit(solution)/shard_map/ppermute | solution.py:234
  81.4 1.2 %collective-permute-start.5 = (f32[4,64]{1,0:T(4,128)S(1)}, f32[4,64]{1,0:T(4,128)S(1)}, u32[]{:S(2)}, u32[]{:S(2)}) collective-permute-start(f32[4,64]{1,0:T(4,128)S(1)} %concatenate.6), channel_id=1, source_target_pairs={{0,4},{4,0},{1,5},{5,1},{2,6},{6,2},{3,7},{7,3},{8,12},{12,8},{9,1... | collective-permute-start | bytes 3080 | tf_op jit(solution)/shard_map/ppermute | solution.py:234
  83.3 3.7 %collective-permute-start.6 = (f32[4,64]{1,0:T(4,128)S(1)}, f32[4,64]{1,0:T(4,128)S(1)}, u32[]{:S(2)}, u32[]{:S(2)}) collective-permute-start(f32[4,64]{1,0:T(4,128)S(1)} %pad_add_fusion), channel_id=1, source_target_pairs={{0,1},{1,0},{2,3},{3,2},{4,5},{5,4},{6,7},{7,6},{8,9},{9,8},{10,11... | collective-permute-start | bytes 3080 | tf_op jit(solution)/shard_map/ppermute | solution.py:234
  86.9 4.5 %collective-permute-start.7 = (f32[4,64]{1,0:T(4,128)S(1)}, f32[4,64]{1,0:T(4,128)S(1)}, u32[]{:S(2)}, u32[]{:S(2)}) collective-permute-start(f32[4,64]{1,0:T(4,128)S(1)} %add.150), channel_id=1, source_target_pairs={{0,2},{1,3},{2,0},{3,1},{4,6},{5,7},{6,4},{7,5},{8,10},{9,11},{10,... | collective-permute-start | bytes 3080 | tf_op jit(solution)/shard_map/ppermute | solution.py:234
  92.6 6.7 %collective-permute-start.9 = (f32[4,64]{1,0:T(4,128)S(1)}, f32[4,64]{1,0:T(4,128)S(1)}, u32[]{:S(2)}, u32[]{:S(2)}) collective-permute-start(f32[4,64]{1,0:T(4,128)S(1)} %concatenate.7), channel_id=1, source_target_pairs={{0,8},{8,16},{16,24},{1,9},{9,17},{17,25},{2,10},{10,18},{18,26},{... | collective-permute-start | bytes 3080 | tf_op jit(solution)/shard_map/ppermute | solution.py:171
  96.7 5.5 %collective-permute-start.8 = (f32[4,64]{1,0:T(4,128)S(1)}, f32[4,64]{1,0:T(4,128)S(1)}, u32[]{:S(2)}, u32[]{:S(2)}) collective-permute-start(f32[4,64]{1,0:T(4,128)S(1)} %concatenate.7), channel_id=1, source_target_pairs={{8,0},{16,8},{24,16},{9,1},{17,9},{25,17},{10,2},{18,10},{26,18},{... | collective-permute-start | bytes 3080 | tf_op jit(solution)/shard_map/ppermute | solution.py:171

commit v3 on v2

--- a/solution.py
+++ b/solution.py
@@ -179,23 +179,50 @@
     return (species_mask, strength)
 
 
-def nonlocal_terms(proj_sums, occupied, strength):
-    band_count = occupied.shape[0]
-    atom_count = strength.shape[0]
-    intersect = proj_sums[:, :band_count]
-    weighted = intersect * occupied[None, :]
-    energy_part = jnp.sum(strength.reshape(-1) * jnp.sum(weighted * intersect, axis=1))
-    forces = []
-    for axis_num in range(3):
-        slope = proj_sums[:, (axis_num + 1) * band_count : (axis_num + 2) * band_count]
-        per_row = jnp.sum(weighted * slope, axis=1).reshape(atom_count, PMAX)
-        forces.append(-2.0 * jnp.sum(strength * per_row, axis=1))
-    return (energy_part, jnp.stack(forces, axis=0))
-
-
-def neb_project(
-    force, here, prev_pos, next_pos, energy, prev_energy, next_energy, tangent_kind, is_climb
+def total(array):
+    return jnp.sum(array, axis=(0, 1), keepdims=True)
+
+
+def terms_kernel(first_ref, sums_ref, occ_ref, strength_ref, out_ref):
+    bands = occ_ref.shape[1]
+    rows, atoms = sums_ref.shape[0], out_ref.shape[1]
+    becp = sums_ref[:, :bands]
+    weighted = becp * occ_ref[...]
+    strength = strength_ref[...]
+    row_atom = (first_ref[0] + lax.broadcasted_iota(jnp.int32, (rows, atoms), 0)) // PMAX
+    mine = row_atom == lax.broadcasted_iota(jnp.int32, (rows, atoms), 1)
+    for c in range(3):
+        slope = sums_ref[:, (c + 1) * bands : (c + 2) * bands]
+        per_row = strength * jnp.sum(weighted * slope, axis=1, keepdims=True)
+        placed = jnp.where(mine, per_row, 0.0)
+        out_ref[c : c + 1, :] = -2.0 * jnp.sum(placed, axis=0, keepdims=True)
+    energy = total(strength * jnp.sum(weighted * becp, axis=1, keepdims=True))
+    out_ref[3:4, :] = jnp.broadcast_to(energy, (1, atoms))
+
+
+def nonlocal_terms(proj_sums, first_row, occupied, strength_rows):
+    vmem = pl.BlockSpec(memory_space=pltpu.VMEM)
+    return pl.pallas_call(
+        terms_kernel,
+        in_specs=[pl.BlockSpec(memory_space=pltpu.SMEM), vmem, vmem, vmem],
+        out_specs=vmem,
+        out_shape=jax.ShapeDtypeStruct((4, ATOMS), jnp.float32),
+        name="terms",
+    )(first_row[None], proj_sums, occupied, strength_rows)
+
+
+def project_kernel(
+    flags_ref, ends_ref, sent_ref, nl_ref, rest_ref, before_ref, after_ref, endpos_ref, out_ref
 ):
+    at_start, at_end = flags_ref[0] == 1, flags_ref[1] == 1
+    is_climb, kind = flags_ref[2] == 1, flags_ref[3]
+    here = sent_ref[:3, :]
+    energy = sent_ref[3:4, :1]
+    force = rest_ref[...] + nl_ref[:3, :]
+    prev_pos = jnp.where(at_start, endpos_ref[0], before_ref[:3, :])
+    next_pos = jnp.where(at_end, endpos_ref[1], after_ref[:3, :])
+    prev_energy = jnp.where(at_start, ends_ref[0], before_ref[3:4, :1])
+    next_energy = jnp.where(at_end, ends_ref[1], after_ref[3:4, :1])
     to_next = next_pos - here
     from_prev = here - prev_pos
     rise_next = jnp.abs(next_energy - energy)
@@ -207,26 +234,33 @@
     weight_prev = 1.0 + jnp.where(rising, smaller, larger)
     stiff_next = spring_constant * (1.0 + jax.nn.sigmoid(0.5 * (next_energy + energy)))
     stiff_prev = spring_constant * (1.0 + jax.nn.sigmoid(0.5 * (prev_energy + energy)))
-    length_next = jnp.sqrt(jnp.sum(to_next * to_next, axis=(1, 2)) + 1.0)
-    length_prev = jnp.sqrt(jnp.sum(from_prev * from_prev, axis=(1, 2)) + 1.0)
-    upwind = weight_next[:, None, None] * to_next + weight_prev[:, None, None] * from_prev
-    forward = to_next / length_next[:, None, None]
-    backward = from_prev / length_prev[:, None, None]
-    kind = tangent_kind[:, None, None]
+    length_next = jnp.sqrt(total(to_next * to_next) + 1.0)
+    length_prev = jnp.sqrt(total(from_prev * from_prev) + 1.0)
+    upwind = weight_next * to_next + weight_prev * from_prev
+    forward = to_next / length_next
+    backward = from_prev / length_prev
     tangent = jnp.where(
         kind == 0,
         upwind,
         jnp.where(kind == 1, forward + backward, jnp.where(kind == 2, forward, backward)),
     )
-    unit_tangent = tangent / jnp.sqrt(jnp.sum(tangent * tangent, axis=(1, 2)) + 1.0)[:, None, None]
-    along = jnp.sum(force * unit_tangent, axis=(1, 2))[:, None, None]
-    climbing = force - 2.0 * along * unit_tangent
-    regular = (
-        force
-        - along * unit_tangent
-        + (stiff_next * length_next - stiff_prev * length_prev)[:, None, None] * unit_tangent
-    )
-    return jnp.where(is_climb[:, None, None], climbing, regular)
+    unit_tangent = tangent / jnp.sqrt(total(tangent * tangent) + 1.0)
+    along = total(force * unit_tangent)
+    spring = stiff_next * length_next - stiff_prev * length_prev
+    scale = jnp.where(is_climb, -2.0 * along, spring - along)
+    out_ref[...] = force + scale * unit_tangent
+
+
+def neb_project(flags, end_energy, sent, packed, force_rest, before, after, end_positions):
+    vmem = pl.BlockSpec(memory_space=pltpu.VMEM)
+    smem = pl.BlockSpec(memory_space=pltpu.SMEM)
+    return pl.pallas_call(
+        project_kernel,
+        in_specs=[smem, smem] + [vmem] * 6,
+        out_specs=vmem,
+        out_shape=jax.ShapeDtypeStruct((3, ATOMS), jnp.float32),
+        name="project",
+    )(flags, end_energy, sent, packed, force_rest, before, after, end_positions)
 
 
 def swapped(array, axis, mask):
@@ -259,7 +293,7 @@
         kept = lax.dynamic_slice_in_dim(rows, bit * half, half, 0)
         sent = lax.dynamic_slice_in_dim(rows, (1 - bit) * half, half, 0)
         rows = kept + swapped(sent, axis, mask)
-        first = first + bit * half
+        first = first + (bit * half).astype(jnp.int32)
         mask *= 2
     return rows, first
 
@@ -310,45 +344,29 @@
         other = other + other_sums
     sums = mine + swapped(other, "band", 1)
     proj_sums, first_row = scattered_rows(sums, "ga")
-    first_local = first_row // PMAX
-    local_atoms = proj_sums.shape[0] // PMAX
-    strength_part = lax.dynamic_slice_in_dim(strength, first_local, local_atoms, 0)
-    energy_part, force_part = nonlocal_terms(proj_sums, occupation[0], strength_part)
-    force_full = lax.dynamic_update_slice_in_dim(
-        jnp.zeros((3, ATOMS), jnp.float32), force_part, first_local, 1
-    )
-    packed = jnp.concatenate(
-        [force_full, jnp.full((1, ATOMS), energy_part, jnp.float32)], axis=0
-    )
+    strength_rows = lax.dynamic_slice_in_dim(
+        strength.reshape(ATOMS * PMAX, 1), first_row, proj_sums.shape[0], 0
+    )
+    packed = nonlocal_terms(proj_sums, first_row, occupation, strength_rows)
     packed = summed(summed(packed, "band"), "ga")
-    energy = energy_rest + packed[3, :1]
-    force = force_rest + packed[None, :3, :]
-    image_index = lax.axis_index("image")
-    image_count = lax.axis_size("image")
-    sent = jnp.concatenate([positions[0], jnp.broadcast_to(energy[:, None], (1, ATOMS))], axis=0)
+    padded = jnp.concatenate([positions[0], jnp.zeros((1, ATOMS), jnp.float32)], axis=0)
+    is_last = lax.broadcasted_iota(jnp.int32, padded.shape, 0) == 3
+    sent = jnp.where(is_last, packed + energy_rest, padded)
     before = passed_along(sent, "image", 1)
     after = passed_along(sent, "image", -1)
-    prev_pos, prev_energy = before[None, :3, :], before[3, :1]
-    next_pos, next_energy = after[None, :3, :], after[3, :1]
-    at_start = image_index == 0
-    at_end = image_index == image_count - 1
-    prev_pos = jnp.where(at_start, end_positions[:1], prev_pos)
-    prev_energy = jnp.where(at_start, end_energy[:1], prev_energy)
-    next_pos = jnp.where(at_end, end_positions[1:], next_pos)
-    next_energy = jnp.where(at_end, end_energy[1:], next_energy)
-    is_climb = climb_index == image_index
+    image_index = lax.axis_index("image")
+    flags = jnp.stack(
+        [
+            (image_index == 0).astype(jnp.int32),
+            (image_index == lax.axis_size("image") - 1).astype(jnp.int32),
+            (climb_index[0] == image_index).astype(jnp.int32),
+            tangent_kind[0],
+        ]
+    )
     neb_force = neb_project(
-        force,
-        positions,
-        prev_pos,
-        next_pos,
-        energy,
-        prev_energy,
-        next_energy,
-        tangent_kind,
-        is_climb,
-    )
-    return (neb_force, energy)
+        flags, end_energy, sent, packed, force_rest[0], before, after, end_positions
+    )
+    return (neb_force[None], sent[3, :1])
 
 
 def solution(mesh):

time: 112 us -> 105 us (0.938)
  between operations: 10.1 us -> 2.86 us
  Pallas kernels: 43.9 us -> 48.2 us
  other arithmetic: 14 us -> 11.3 us
    pallas_call x0 -> x2, Pallas kernels: none -> 3.78 us  [the longest x1 1.95 us: nonlocal_terms(): pl.pallas_call(terms_kernel, in_specs=[pl.BlockSpec(memory_space=pltpu.SM...]
    reduce_sum x6 -> x0, other arithmetic: 3.46 us -> none  [the longest x1 0.69 us: neb_project(): jnp.sum(tangent * tangent, axis=(1, 2)) + 1.0]
    unnamed x23 -> x28, local copies, waits for them, and re-layouts: 4.25 us -> 7.28 us
    slice x4 -> x1, local copies, waits for them, and re-layouts: 2.21 us -> 0.51 us  [per_device(): return (neb_force[None], sent[3, :1])]
    ppermute x8, waiting for transfers between devices: 13.4 us -> 11.8 us  [swapped(): return lax.ppermute(array, axis, pairs)]
  transfers between devices with their start and end apart: 10 -> 10, of which waited for: 8 -> 7; matrix products, arithmetic and copies ran while one was open for 6% -> 8% of each run, Pallas kernels for 20% -> 21%
where the time goes in v3:
time: 105 us
  Pallas kernels  48.2 us (46%)
  starting transfers between devices  15.8 us (15%)
  local copies, waits for them, and re-layouts  13.7 us (13%)
  waiting for transfers between devices  13.7 us (13%)
  other arithmetic  11.3 us (11%)
  between operations  2.86 us (3%)
    pallas_call x2, Pallas kernels, contract(): pl.pallas_call(functools.partial(contract_kernel, parts=parts, gc=gc, rb=...  44.4 us
    ppermute x8, waiting for transfers between devices, swapped(): return lax.ppermute(array, axis, pairs)  11.8 us
    ppermute x8, starting transfers between devices, swapped(): return lax.ppermute(array, axis, pairs)  11.2 us
    convert_element_type x1, other arithmetic, per_device(): given = rows_of((1 - core) * half + at, count).astype(jnp.float32)  8.51 us
    unnamed x28, local copies, waits for them, and re-layouts  7.28 us
    convert_element_type x2, local copies, waits for them, and re-layouts, per_device(): given = rows_of((1 - core) * half + at, count).astype(jnp.float32)  4.86 us
    ppermute x2, starting transfers between devices, passed_along(): return lax.ppermute(array, axis, pairs)  4.67 us
  transfers between devices with their start and end apart: 10, of which 7 were waited for; matrix products, arithmetic and copies ran while one was open for 8% of the time, Pallas kernels for 21%

profile of v3, /device:TPU:0, one launch (start us, length us, event | category | flops | bytes accessed | tf_op | source)
XLA Modules:
  0.0 105.5 jit_solution(9940205207120803807)
XLA Ops:
  0.7 8.5 %convert_bitcast_fusion = (f32[2,32,16384]{2,0,1:T(2,128)S(1)}, bf16[1,32,2,16384]{3,2,1,0:T(2,128)(2,1)S(1)}, bf16[1,32,2,16384]{3,2,1,0:T(2,128)(2,1)S(1)}, f32[2,32,16384]{2,0,1:T(2,128)S(1)}) fusion(bf16[1,32,2,65536]{3,2,1,0:T(2,128)(2,1)} %param.14, s32[]{:T(128)S(6)} %select_n.58, s32[]{:T(128)S(6)} %select_n.55, s32[]{:T(128)S(6)} %select_n.57, ...), kind=kLoop, calls=%fused_computation | loop fusion | flops 2097152 | bytes 20971536 | tf_op jit(solution)/shard_map/convert_element_type | solution.py:333
  9.2 2.4 %copy.30 = f32[2,32,16384]{2,1,0:T(8,128)S(1)} copy(f32[2,32,16384]{2,0,1:T(2,128)S(1)} %get-tuple-element.18) | data formatting | bytes 8388608 | tf_op jit(solution)/shard_map/convert_element_type | solution.py:333
  12.2 2.4 %copy.28 = f32[2,32,16384]{2,1,0:T(8,128)S(1)} copy(f32[2,32,16384]{2,0,1:T(2,128)S(1)} %get-tuple-element.21) | data formatting | bytes 8388608 | tf_op jit(solution)/shard_map/convert_element_type | solution.py:333
  14.7 1.2 %copy.38 = bf16[1,32,2,16384]{3,1,2,0:T(8,128)(2,1)S(1)} copy(bf16[1,32,2,16384]{3,2,1,0:T(2,128)(2,1)S(1)} %get-tuple-element.20) | data formatting | bytes 4194304
  15.9 1.2 %copy.37 = bf16[1,32,2,16384]{3,1,2,0:T(8,128)(2,1)S(1)} copy(bf16[1,32,2,16384]{3,2,1,0:T(2,128)(2,1)S(1)} %get-tuple-element.19) | data formatting | bytes 4194304
  17.2 1.8 %collective-permute-done.1.refs_7_ = f32[64,16384]{1,0:T(8,128)S(1)} collective-permute-done((f32[64,16384]{1,0:T(8,128)S(1)}, f32[64,16384]{1,0:T(8,128)S(1)}, u32[]{:S(2)}, u32[]{:S(2)}) %collective-permute-start.1) | collective-permute-done | bytes 4194336 | tf_op jit(solution)/shard_map/ppermute | solution.py:268
  19.1 1.9 %copy-done.10 = f32[64,16384]{1,0:T(8,128)} copy-done((f32[64,16384]{1,0:T(8,128)}, f32[64,16384]{1,0:T(8,128)S(1)}, u32[]{:S(2)}) %copy-start.10) | copy-done | bytes 4194328
  21.0 22.3 %contract.3 = (f32[512,128]{1,0:T(8,128)S(1)}, f32[512,128]{1,0:T(8,128)S(1)}) custom-call(s32[64]{0:T(128)S(1)} %copy-done, s32[1]{0:T(128)} %bitcast.12.refs_1_, f32[4,8,65536]{2,1,0:T(8,128)} %refs_2_.3, f32[3,65536]{1,0:T(4,128)S(1)} %copy-done.1, f32[3,64,128]{2,1,0:T(8,128)S(1)} %broadcast_in_dim.17.refs_4_, ...), custom_call_target="tpu_custom_call" | custom-call | flops 8589934592 | bytes 4587520 | tf_op jit(solution)/shard_map/contract/pallas_call | solution.py:138
  43.4 22.1 %contract.2 = (f32[512,128]{1,0:T(8,128)S(1)}, f32[512,128]{1,0:T(8,128)S(1)}) custom-call(s32[64]{0:T(128)S(1)} %copy-done, s32[1]{0:T(128)} %bitcast.5.refs_1_, f32[4,8,65536]{2,1,0:T(8,128)} %refs_2_.3, f32[3,65536]{1,0:T(4,128)S(1)} %copy-done.1, f32[3,64,128]{2,1,0:T(8,128)S(1)} %broadcast_in_dim.17.refs_4_, f32[4,8,128]{2,1,0:T(8,128)S(1)} %broadcast_in_dim.18.refs_5_, ...), custom_call_target="tpu_custom_call" | custom-call | flops 8589934592 | bytes 4587520 | tf_op jit(solution)/shard_map/contract/pallas_call | solution.py:138
  66.0 1.2 %collective-permute-done.2 = f32[512,128]{1,0:T(8,128)S(1)} collective-permute-done((f32[512,128]{1,0:T(8,128)S(1)}, f32[512,128]{1,0:T(8,128)S(1)}, u32[]{:S(2)}, u32[]{:S(2)}) %collective-permute-start.2) | collective-permute-done | bytes 262176 | tf_op jit(solution)/shard_map/ppermute | solution.py:268
  67.2 3.0 %collective-permute-start.3 = (f32[256,128]{1,0:T(8,128)S(1)}, f32[256,128]{1,0:T(8,128)S(1)}, u32[]{:S(2)}, u32[]{:S(2)}) collective-permute-start(f32[256,128]{1,0:T(8,128)S(1)} %constant_dynamic-slice_fusion.2), channel_id=1, source_target_pairs={{0,1},{1,0},{2,3},{3,2},{4,5},{5,4},{6,7},{7,6},{8,9},{9,8},{10,11... | collective-permute-start | bytes 393224 | tf_op jit(solution)/shard_map/ppermute | solution.py:268
  70.5 3.5 %collective-permute-done.3 = f32[256,128]{1,0:T(8,128)S(1)} collective-permute-done((f32[256,128]{1,0:T(8,128)S(1)}, f32[256,128]{1,0:T(8,128)S(1)}, u32[]{:S(2)}, u32[]{:S(2)}) %collective-permute-start.3) | collective-permute-done | bytes 131104 | tf_op jit(solution)/shard_map/ppermute | solution.py:268
  74.0 2.8 %collective-permute-start.4 = (f32[128,128]{1,0:T(8,128)S(1)}, f32[128,128]{1,0:T(8,128)S(1)}, u32[]{:S(2)}, u32[]{:S(2)}) collective-permute-start(f32[128,128]{1,0:T(8,128)S(1)} %constant_dynamic-slice_fusion.1), channel_id=1, source_target_pairs={{0,2},{1,3},{2,0},{3,1},{4,6},{5,7},{6,4},{7,5},{8,10},{9,11},{10,... | collective-permute-start | bytes 196616 | tf_op jit(solution)/shard_map/ppermute | solution.py:268
  76.9 0.6 constant_dynamic-slice_fusion.strength_ref
  77.5 2.0 %collective-permute-done.4 = f32[128,128]{1,0:T(8,128)S(1)} collective-permute-done((f32[128,128]{1,0:T(8,128)S(1)}, f32[128,128]{1,0:T(8,128)S(1)}, u32[]{:S(2)}, u32[]{:S(2)}) %collective-permute-start.4) | collective-permute-done | bytes 65568 | tf_op jit(solution)/shard_map/ppermute | solution.py:268
  79.5 0.6 dynamic-slice_add_fusion.1.sums_ref
  80.1 1.9 %terms.1 = f32[4,64]{1,0:T(4,128)} custom-call(s32[1]{0:T(128)} %bitcast.4.first_ref, f32[128,128]{1,0:T(8,128)} %dynamic-slice_add_fusion.1.sums_ref, f32[1,32]{1,0:T(1,128)} %occ_ref.1, f32[128,1]{1,0:T(8,128)} %constant_dynamic-slice_fusion.strength_ref), custom_call_target="tpu_custom_call" | custom-call | tf_op jit(solution)/shard_map/terms/pallas_call | solution.py:205
  82.0 1.4 %collective-permute-done.5 = f32[4,64]{1,0:T(4,128)S(1)} collective-permute-done((f32[4,64]{1,0:T(4,128)}, f32[4,64]{1,0:T(4,128)S(1)}, u32[]{:S(2)}, u32[]{:S(2)}) %collective-permute-start.5) | collective-permute-done | bytes 1056 | tf_op jit(solution)/shard_map/ppermute | solution.py:268
  83.4 0.7 add.104
  84.1 1.6 %collective-permute-start.6 = (f32[4,64]{1,0:T(4,128)S(1)}, f32[4,64]{1,0:T(4,128)S(1)}, u32[]{:S(2)}, u32[]{:S(2)}) collective-permute-start(f32[4,64]{1,0:T(4,128)S(1)} %add.104), channel_id=1, source_target_pairs={{0,1},{1,0},{2,3},{3,2},{4,5},{5,4},{6,7},{7,6},{8,9},{9,8},{10,11... | collective-permute-start | bytes 3080 | tf_op jit(solution)/shard_map/ppermute | solution.py:268
  85.6 2.0 %collective-permute-done.6 = f32[4,64]{1,0:T(4,128)S(1)} collective-permute-done((f32[4,64]{1,0:T(4,128)S(1)}, f32[4,64]{1,0:T(4,128)S(1)}, u32[]{:S(2)}, u32[]{:S(2)}) %collective-permute-start.6) | collective-permute-done | bytes 1056 | tf_op jit(solution)/shard_map/ppermute | solution.py:268
  87.7 2.7 %collective-permute-start.7 = (f32[4,64]{1,0:T(4,128)S(1)}, f32[4,64]{1,0:T(4,128)S(1)}, u32[]{:S(2)}, u32[]{:S(2)}) collective-permute-start(f32[4,64]{1,0:T(4,128)S(1)} %add.105), channel_id=1, source_target_pairs={{0,2},{1,3},{2,0},{3,1},{4,6},{5,7},{6,4},{7,5},{8,10},{9,11},{10,... | collective-permute-start | bytes 3080 | tf_op jit(solution)/shard_map/ppermute | solution.py:268
  92.3 0.6 pad_select_fusion
  92.9 3.4 %collective-permute-start.8 = (f32[4,64]{1,0:T(4,128)S(1)}, f32[4,64]{1,0:T(4,128)S(1)}, u32[]{:S(2)}, u32[]{:S(2)}) collective-permute-start(f32[4,64]{1,0:T(4,128)S(1)} %get-tuple-element.16.sent_ref), channel_id=1, source_target_pairs={{0,8},{8,16},{16,24},{1,9},{9,17},{17,25},{2,10},{10,18},{18,26},{... | collective-permute-start | bytes 3080 | tf_op jit(solution)/shard_map/ppermute | solution.py:171
  96.3 1.3 %collective-permute-start.9 = (f32[4,64]{1,0:T(4,128)S(1)}, f32[4,64]{1,0:T(4,128)S(1)}, u32[]{:S(2)}, u32[]{:S(2)}) collective-permute-start(f32[4,64]{1,0:T(4,128)S(1)} %get-tuple-element.16.sent_ref), channel_id=1, source_target_pairs={{8,0},{16,8},{24,16},{9,1},{17,9},{25,17},{10,2},{18,10},{26,18},{... | collective-permute-start | bytes 3080 | tf_op jit(solution)/shard_map/ppermute | solution.py:171
  97.6 0.6 pad_add_fusion.flags_ref
  98.2 0.6 copy.33.endpos_ref
  98.8 0.6 copy.41
  99.9 1.9 %collective-permute-done.9.after_ref = f32[4,64]{1,0:T(4,128)S(1)} collective-permute-done((f32[4,64]{1,0:T(4,128)S(1)}, f32[4,64]{1,0:T(4,128)S(1)}, u32[]{:S(2)}, u32[]{:S(2)}) %collective-permute-start.9) | collective-permute-done | bytes 1056 | tf_op jit(solution)/shard_map/ppermute | solution.py:171
  101.8 0.6 copy-done.6
  102.4 1.8 %project.1 = f32[3,64]{1,0:T(4,128)} custom-call(s32[4]{0:T(128)} %pad_add_fusion.flags_ref, f32[2]{0:T(128)} %ends_ref.1, f32[4,64]{1,0:T(4,128)} %copy-done.2, f32[4,64]{1,0:T(4,128)} %get-tuple-element.17.nl_ref, f32[3,64]{1,0:T(4,128)} %bitcast.46, f32[4,64]{1,0:T(4,128)} %copy-done.5, f32[4,64]{1,0:T(4,128)} %copy-done.6, f32[2,3,64]{2,1,0:T(4,128)} %copy.33.endpos_ref), custom_call_target="tpu_custom_call" | custom-call | tf_op jit(solution)/shard_map/project/pallas_call | solution.py:257
  104.2 1.2 %copy.34 = f32[1,3,64]{2,0,1:T(1,128)} copy(f32[1,3,64]{2,1,0:T(4,128)} %bitcast.47) | data formatting | bytes 1536
  (43 shorter events, 2.3 us)
Async XLA Ops:
  11.6 7.3 %collective-permute-start.1 = (f32[64,16384]{1,0:T(8,128)S(1)}, f32[64,16384]{1,0:T(8,128)S(1)}, u32[]{:S(2)}, u32[]{:S(2)}) collective-permute-start(f32[64,16384]{1,0:T(8,128)S(1)} %bitcast.43), channel_id=1, source_target_pairs={{0,4},{4,0},{1,5},{5,1},{2,6},{6,2},{3,7},{7,3},{8,12},{12,8},{9,1... | collective-permute-start | bytes 12582920 | tf_op jit(solution)/shard_map/ppermute | solution.py:268
  14.6 1.3 %copy-start.7 = (f32[1,3,64]{2,0,1:T(1,128)S(1)}, f32[1,3,64]{2,0,1:T(1,128)}, u32[]{:S(2)}) copy-start(f32[1,3,64]{2,0,1:T(1,128)} %param.21) | copy-start | bytes 2308
  14.6 28.7 %collective-permute-start = (f32[64,16384]{1,0:T(8,128)S(1)}, f32[64,16384]{1,0:T(8,128)}, u32[]{:S(2)}, u32[]{:S(2)}) collective-permute-start(f32[64,16384]{1,0:T(8,128)S(1)} %bitcast.42), channel_id=1, source_target_pairs={{0,4},{4,0},{1,5},{5,1},{2,6},{6,2},{3,7},{7,3},{8,12},{12,8},{9,1... | collective-permute-start | bytes 12582920 | tf_op jit(solution)/shard_map/ppermute | solution.py:268
  14.7 2.4 %copy-start.9 = (s32[4]{0:T(128)S(1)}, s32[4]{0:T(128)}, u32[]{:S(2)}) copy-start(s32[4]{0:T(128)} %param.19) | copy-start | bytes 52
  14.7 6.3 %copy-start = (s32[64]{0:T(128)S(1)}, s32[64]{0:T(128)}, u32[]{:S(2)}) copy-start(s32[64]{0:T(128)} %refs_0_.3) | copy-start | bytes 772
  14.7 6.3 %copy-start.1 = (f32[3,65536]{1,0:T(4,128)S(1)}, f32[3,65536]{1,0:T(4,128)}, u32[]{:S(2)}) copy-start(f32[3,65536]{1,0:T(4,128)} %refs_3_.3) | copy-start | bytes 2359300
  19.0 2.0 %copy-start.10 = (f32[64,16384]{1,0:T(8,128)}, f32[64,16384]{1,0:T(8,128)S(1)}, u32[]{:S(2)}) copy-start(f32[64,16384]{1,0:T(8,128)S(1)} %collective-permute-done.1.refs_7_) | copy-start | bytes 12582916
  43.3 26.9 %copy-start.4 = (f32[4,8]{1,0:T(4,128)S(1)}, f32[4,8]{1,0:T(4,128)}, u32[]{:S(2)}) copy-start(f32[4,8]{1,0:T(4,128)} %param.20) | copy-start | bytes 388
  43.3 54.9 %copy-start.3 = (f32[2,3,64]{2,0,1:T(2,128)S(1)}, f32[2,3,64]{2,0,1:T(2,128)}, u32[]{:S(2)}) copy-start(f32[2,3,64]{2,0,1:T(2,128)} %param.24) | copy-start | bytes 4612
  43.4 55.5 %copy-start.8 = (f32[1,3,64]{2,0,1:T(1,128)S(1)}, f32[1,3,64]{2,0,1:T(1,128)}, u32[]{:S(2)}) copy-start(f32[1,3,64]{2,0,1:T(1,128)} %param.23) | copy-start | bytes 2308
  65.5 1.6 %collective-permute-start.2 = (f32[512,128]{1,0:T(8,128)S(1)}, f32[512,128]{1,0:T(8,128)S(1)}, u32[]{:S(2)}, u32[]{:S(2)}) collective-permute-start(f32[512,128]{1,0:T(8,128)S(1)} %add.95), channel_id=1, source_target_pairs={{0,4},{4,0},{1,5},{5,1},{2,6},{6,2},{3,7},{7,3},{8,12},{12,8},{9,1... | collective-permute-start | bytes 786440 | tf_op jit(solution)/shard_map/ppermute | solution.py:268
  67.2 6.8 %collective-permute-start.3 = (f32[256,128]{1,0:T(8,128)S(1)}, f32[256,128]{1,0:T(8,128)S(1)}, u32[]{:S(2)}, u32[]{:S(2)}) collective-permute-start(f32[256,128]{1,0:T(8,128)S(1)} %constant_dynamic-slice_fusion.2), channel_id=1, source_target_pairs={{0,1},{1,0},{2,3},{3,2},{4,5},{5,4},{6,7},{7,6},{8,9},{9,8},{10,11... | collective-permute-start | bytes 393224 | tf_op jit(solution)/shard_map/ppermute | solution.py:268
  74.0 5.4 %collective-permute-start.4 = (f32[128,128]{1,0:T(8,128)S(1)}, f32[128,128]{1,0:T(8,128)S(1)}, u32[]{:S(2)}, u32[]{:S(2)}) collective-permute-start(f32[128,128]{1,0:T(8,128)S(1)} %constant_dynamic-slice_fusion.1), channel_id=1, source_target_pairs={{0,2},{1,3},{2,0},{3,1},{4,6},{5,7},{6,4},{7,5},{8,10},{9,11},{10,... | collective-permute-start | bytes 196616 | tf_op jit(solution)/shard_map/ppermute | solution.py:268
  82.0 1.4 %collective-permute-start.5 = (f32[4,64]{1,0:T(4,128)}, f32[4,64]{1,0:T(4,128)S(1)}, u32[]{:S(2)}, u32[]{:S(2)}) collective-permute-start(f32[4,64]{1,0:T(4,128)} %terms.1), channel_id=1, source_target_pairs={{0,4},{4,0},{1,5},{5,1},{2,6},{6,2},{3,7},{7,3},{8,12},{12,8},{9,1... | collective-permute-start | bytes 3080 | tf_op jit(solution)/shard_map/ppermute | solution.py:268
  84.1 3.6 %collective-permute-start.6 = (f32[4,64]{1,0:T(4,128)S(1)}, f32[4,64]{1,0:T(4,128)S(1)}, u32[]{:S(2)}, u32[]{:S(2)}) collective-permute-start(f32[4,64]{1,0:T(4,128)S(1)} %add.104), channel_id=1, source_target_pairs={{0,1},{1,0},{2,3},{3,2},{4,5},{5,4},{6,7},{7,6},{8,9},{9,8},{10,11... | collective-permute-start | bytes 3080 | tf_op jit(solution)/shard_map/ppermute | solution.py:268
  87.7 4.7 %collective-permute-start.7 = (f32[4,64]{1,0:T(4,128)S(1)}, f32[4,64]{1,0:T(4,128)S(1)}, u32[]{:S(2)}, u32[]{:S(2)}) collective-permute-start(f32[4,64]{1,0:T(4,128)S(1)} %add.105), channel_id=1, source_target_pairs={{0,2},{1,3},{2,0},{3,1},{4,6},{5,7},{6,4},{7,5},{8,10},{9,11},{10,... | collective-permute-start | bytes 3080 | tf_op jit(solution)/shard_map/ppermute | solution.py:268
  92.9 8.9 %copy-start.2 = (f32[4,64]{1,0:T(4,128)}, f32[4,64]{1,0:T(4,128)S(1)}, u32[]{:S(2)}) copy-start(f32[4,64]{1,0:T(4,128)S(1)} %get-tuple-element.16.sent_ref) | copy-start | bytes 3076
  92.9 7.0 %collective-permute-start.8 = (f32[4,64]{1,0:T(4,128)S(1)}, f32[4,64]{1,0:T(4,128)S(1)}, u32[]{:S(2)}, u32[]{:S(2)}) collective-permute-start(f32[4,64]{1,0:T(4,128)S(1)} %get-tuple-element.16.sent_ref), channel_id=1, source_target_pairs={{0,8},{8,16},{16,24},{1,9},{9,17},{17,25},{2,10},{10,18},{18,26},{... | collective-permute-start | bytes 3080 | tf_op jit(solution)/shard_map/ppermute | solution.py:171
  96.3 5.5 %collective-permute-start.9 = (f32[4,64]{1,0:T(4,128)S(1)}, f32[4,64]{1,0:T(4,128)S(1)}, u32[]{:S(2)}, u32[]{:S(2)}) collective-permute-start(f32[4,64]{1,0:T(4,128)S(1)} %get-tuple-element.16.sent_ref), channel_id=1, source_target_pairs={{8,0},{16,8},{24,16},{9,1},{17,9},{25,17},{10,2},{18,10},{26,18},{... | collective-permute-start | bytes 3080 | tf_op jit(solution)/shard_map/ppermute | solution.py:171
  99.9 1.9 %copy-start.5 = (f32[4,64]{1,0:T(4,128)}, f32[4,64]{1,0:T(4,128)S(1)}, u32[]{:S(2)}) copy-start(f32[4,64]{1,0:T(4,128)S(1)} %collective-permute-done.8.before_ref) | copy-start | bytes 3076
  101.8 0.6 copy-start.6

commit v4 on v3

--- a/solution.py
+++ b/solution.py
@@ -248,7 +248,7 @@
     along = total(force * unit_tangent)
     spring = stiff_next * length_next - stiff_prev * length_prev
     scale = jnp.where(is_climb, -2.0 * along, spring - along)
-    out_ref[...] = force + scale * unit_tangent
+    out_ref[:, 0, :] = force + scale * unit_tangent
 
 
 def neb_project(flags, end_energy, sent, packed, force_rest, before, after, end_positions):
@@ -258,7 +258,7 @@
         project_kernel,
         in_specs=[smem, smem] + [vmem] * 6,
         out_specs=vmem,
-        out_shape=jax.ShapeDtypeStruct((3, ATOMS), jnp.float32),
+        out_shape=jax.ShapeDtypeStruct((3, 1, ATOMS), jnp.float32),
         name="project",
     )(flags, end_energy, sent, packed, force_rest, before, after, end_positions)
 
@@ -366,7 +366,7 @@
     neb_force = neb_project(
         flags, end_energy, sent, packed, force_rest[0], before, after, end_positions
     )
-    return (neb_force[None], sent[3, :1])
+    return (neb_force.transpose(1, 0, 2), sent[3, :1])
 
 
 def solution(mesh):

time: 105 us -> 104 us (level)
  local copies, waits for them, and re-layouts: 13.7 us -> 12.4 us
    unnamed x28 -> x27, local copies, waits for them, and re-layouts: 7.28 us -> 6.04 us
where the time goes in v4:
time: 104 us
  Pallas kernels  48.1 us (46%)
  starting transfers between devices  15.8 us (15%)
  waiting for transfers between devices  13.6 us (13%)
  local copies, waits for them, and re-layouts  12.4 us (12%)
  other arithmetic  11.3 us (11%)
  between operations  2.86 us (3%)
    pallas_call x2, Pallas kernels, contract(): pl.pallas_call(functools.partial(contract_kernel, parts=parts, gc=gc, rb=...  44.3 us
    ppermute x8, waiting for transfers between devices, swapped(): return lax.ppermute(array, axis, pairs)  11.8 us
    ppermute x8, starting transfers between devices, swapped(): return lax.ppermute(array, axis, pairs)  11.1 us
    convert_element_type x1, other arithmetic, per_device(): given = rows_of((1 - core) * half + at, count).astype(jnp.float32)  8.51 us
    unnamed x27, local copies, waits for them, and re-layouts  6.04 us
    convert_element_type x2, local copies, waits for them, and re-layouts, per_device(): given = rows_of((1 - core) * half + at, count).astype(jnp.float32)  4.86 us
    ppermute x2, starting transfers between devices, passed_along(): return lax.ppermute(array, axis, pairs)  4.67 us
  transfers between devices with their start and end apart: 10, of which 7 were waited for; matrix products, arithmetic and copies ran while one was open for 8% of the time, Pallas kernels for 21%

profile of v4, /device:TPU:0, one launch (start us, length us, event | category | flops | bytes accessed | tf_op | source)
XLA Modules:
  0.0 104.2 jit_solution(735574607971933952)
XLA Ops:
  0.7 8.5 %convert_bitcast_fusion = (f32[2,32,16384]{2,0,1:T(2,128)S(1)}, bf16[1,32,2,16384]{3,2,1,0:T(2,128)(2,1)S(1)}, bf16[1,32,2,16384]{3,2,1,0:T(2,128)(2,1)S(1)}, f32[2,32,16384]{2,0,1:T(2,128)S(1)}) fusion(bf16[1,32,2,65536]{3,2,1,0:T(2,128)(2,1)} %param.14, s32[]{:T(128)S(6)} %select_n.58, s32[]{:T(128)S(6)} %select_n.55, s32[]{:T(128)S(6)} %select_n.57, ...), kind=kLoop, calls=%fused_computation | loop fusion | flops 2097152 | bytes 20971536 | tf_op jit(solution)/shard_map/convert_element_type | solution.py:333
  9.2 2.4 %copy.28 = f32[2,32,16384]{2,1,0:T(8,128)S(1)} copy(f32[2,32,16384]{2,0,1:T(2,128)S(1)} %get-tuple-element.12) | data formatting | bytes 8388608 | tf_op jit(solution)/shard_map/convert_element_type | solution.py:333
  11.6 0.6 collective-permute-start.1
  12.2 2.4 %copy.26 = f32[2,32,16384]{2,1,0:T(8,128)S(1)} copy(f32[2,32,16384]{2,0,1:T(2,128)S(1)} %get-tuple-element.15) | data formatting | bytes 8388608 | tf_op jit(solution)/shard_map/convert_element_type | solution.py:333
  14.7 1.2 %copy.35 = bf16[1,32,2,16384]{3,1,2,0:T(8,128)(2,1)S(1)} copy(bf16[1,32,2,16384]{3,2,1,0:T(2,128)(2,1)S(1)} %get-tuple-element.14) | data formatting | bytes 4194304
  15.9 1.2 %copy.34 = bf16[1,32,2,16384]{3,1,2,0:T(8,128)(2,1)S(1)} copy(bf16[1,32,2,16384]{3,2,1,0:T(2,128)(2,1)S(1)} %get-tuple-element.13) | data formatting | bytes 4194304
  17.2 1.8 %collective-permute-done.1.refs_7_ = f32[64,16384]{1,0:T(8,128)S(1)} collective-permute-done((f32[64,16384]{1,0:T(8,128)S(1)}, f32[64,16384]{1,0:T(8,128)S(1)}, u32[]{:S(2)}, u32[]{:S(2)}) %collective-permute-start.1) | collective-permute-done | bytes 4194336 | tf_op jit(solution)/shard_map/ppermute | solution.py:268
  19.1 1.9 %copy-done.10 = f32[64,16384]{1,0:T(8,128)} copy-done((f32[64,16384]{1,0:T(8,128)}, f32[64,16384]{1,0:T(8,128)S(1)}, u32[]{:S(2)}) %copy-start.10) | copy-done | bytes 4194328
  21.0 22.3 %contract.3 = (f32[512,128]{1,0:T(8,128)S(1)}, f32[512,128]{1,0:T(8,128)S(1)}) custom-call(s32[64]{0:T(128)S(1)} %copy-done, s32[1]{0:T(128)} %bitcast.12.refs_1_, f32[4,8,65536]{2,1,0:T(8,128)} %refs_2_.3, f32[3,65536]{1,0:T(4,128)S(1)} %copy-done.1, f32[3,64,128]{2,1,0:T(8,128)S(1)} %broadcast_in_dim.15.refs_4_, ...), custom_call_target="tpu_custom_call" | custom-call | flops 8589934592 | bytes 4587520 | tf_op jit(solution)/shard_map/contract/pallas_call | solution.py:138
  43.3 22.1 %contract.2 = (f32[512,128]{1,0:T(8,128)S(1)}, f32[512,128]{1,0:T(8,128)S(1)}) custom-call(s32[64]{0:T(128)S(1)} %copy-done, s32[1]{0:T(128)} %bitcast.5.refs_1_, f32[4,8,65536]{2,1,0:T(8,128)} %refs_2_.3, f32[3,65536]{1,0:T(4,128)S(1)} %copy-done.1, f32[3,64,128]{2,1,0:T(8,128)S(1)} %broadcast_in_dim.15.refs_4_, f32[4,8,128]{2,1,0:T(8,128)S(1)} %broadcast_in_dim.16.refs_5_, ...), custom_call_target="tpu_custom_call" | custom-call | flops 8589934592 | bytes 4587520 | tf_op jit(solution)/shard_map/contract/pallas_call | solution.py:138
  65.9 1.2 %collective-permute-done.2 = f32[512,128]{1,0:T(8,128)S(1)} collective-permute-done((f32[512,128]{1,0:T(8,128)S(1)}, f32[512,128]{1,0:T(8,128)S(1)}, u32[]{:S(2)}, u32[]{:S(2)}) %collective-permute-start.2) | collective-permute-done | bytes 262176 | tf_op jit(solution)/shard_map/ppermute | solution.py:268
  67.2 3.0 %collective-permute-start.3 = (f32[256,128]{1,0:T(8,128)S(1)}, f32[256,128]{1,0:T(8,128)S(1)}, u32[]{:S(2)}, u32[]{:S(2)}) collective-permute-start(f32[256,128]{1,0:T(8,128)S(1)} %constant_dynamic-slice_fusion.2), channel_id=1, source_target_pairs={{0,1},{1,0},{2,3},{3,2},{4,5},{5,4},{6,7},{7,6},{8,9},{9,8},{10,11... | collective-permute-start | bytes 393224 | tf_op jit(solution)/shard_map/ppermute | solution.py:268
  70.5 3.5 %collective-permute-done.3 = f32[256,128]{1,0:T(8,128)S(1)} collective-permute-done((f32[256,128]{1,0:T(8,128)S(1)}, f32[256,128]{1,0:T(8,128)S(1)}, u32[]{:S(2)}, u32[]{:S(2)}) %collective-permute-start.3) | collective-permute-done | bytes 131104 | tf_op jit(solution)/shard_map/ppermute | solution.py:268
  74.0 2.8 %collective-permute-start.4 = (f32[128,128]{1,0:T(8,128)S(1)}, f32[128,128]{1,0:T(8,128)S(1)}, u32[]{:S(2)}, u32[]{:S(2)}) collective-permute-start(f32[128,128]{1,0:T(8,128)S(1)} %constant_dynamic-slice_fusion.1), channel_id=1, source_target_pairs={{0,2},{1,3},{2,0},{3,1},{4,6},{5,7},{6,4},{7,5},{8,10},{9,11},{10,... | collective-permute-start | bytes 196616 | tf_op jit(solution)/shard_map/ppermute | solution.py:268
  76.8 0.6 constant_dynamic-slice_fusion.strength_ref
  77.5 2.0 %collective-permute-done.4 = f32[128,128]{1,0:T(8,128)S(1)} collective-permute-done((f32[128,128]{1,0:T(8,128)S(1)}, f32[128,128]{1,0:T(8,128)S(1)}, u32[]{:S(2)}, u32[]{:S(2)}) %collective-permute-start.4) | collective-permute-done | bytes 65568 | tf_op jit(solution)/shard_map/ppermute | solution.py:268
  79.4 0.6 dynamic-slice_add_fusion.1.sums_ref
  80.1 1.9 %terms.1 = f32[4,64]{1,0:T(4,128)} custom-call(s32[1]{0:T(128)} %bitcast.4.first_ref, f32[128,128]{1,0:T(8,128)} %dynamic-slice_add_fusion.1.sums_ref, f32[1,32]{1,0:T(1,128)} %occ_ref.1, f32[128,1]{1,0:T(8,128)} %constant_dynamic-slice_fusion.strength_ref), custom_call_target="tpu_custom_call" | custom-call | tf_op jit(solution)/shard_map/terms/pallas_call | solution.py:205
  82.0 1.4 %collective-permute-done.5 = f32[4,64]{1,0:T(4,128)S(1)} collective-permute-done((f32[4,64]{1,0:T(4,128)}, f32[4,64]{1,0:T(4,128)S(1)}, u32[]{:S(2)}, u32[]{:S(2)}) %collective-permute-start.5) | collective-permute-done | bytes 1056 | tf_op jit(solution)/shard_map/ppermute | solution.py:268
  83.4 0.7 add.104
  84.1 1.5 %collective-permute-start.6 = (f32[4,64]{1,0:T(4,128)S(1)}, f32[4,64]{1,0:T(4,128)S(1)}, u32[]{:S(2)}, u32[]{:S(2)}) collective-permute-start(f32[4,64]{1,0:T(4,128)S(1)} %add.104), channel_id=1, source_target_pairs={{0,1},{1,0},{2,3},{3,2},{4,5},{5,4},{6,7},{7,6},{8,9},{9,8},{10,11... | collective-permute-start | bytes 3080 | tf_op jit(solution)/shard_map/ppermute | solution.py:268
  85.6 2.0 %collective-permute-done.6 = f32[4,64]{1,0:T(4,128)S(1)} collective-permute-done((f32[4,64]{1,0:T(4,128)S(1)}, f32[4,64]{1,0:T(4,128)S(1)}, u32[]{:S(2)}, u32[]{:S(2)}) %collective-permute-start.6) | collective-permute-done | bytes 1056 | tf_op jit(solution)/shard_map/ppermute | solution.py:268
  87.7 2.7 %collective-permute-start.7 = (f32[4,64]{1,0:T(4,128)S(1)}, f32[4,64]{1,0:T(4,128)S(1)}, u32[]{:S(2)}, u32[]{:S(2)}) collective-permute-start(f32[4,64]{1,0:T(4,128)S(1)} %add.105), channel_id=1, source_target_pairs={{0,2},{1,3},{2,0},{3,1},{4,6},{5,7},{6,4},{7,5},{8,10},{9,11},{10,... | collective-permute-start | bytes 3080 | tf_op jit(solution)/shard_map/ppermute | solution.py:268
  92.3 0.6 pad_select_fusion
  92.9 3.4 %collective-permute-start.8 = (f32[4,64]{1,0:T(4,128)S(1)}, f32[4,64]{1,0:T(4,128)S(1)}, u32[]{:S(2)}, u32[]{:S(2)}) collective-permute-start(f32[4,64]{1,0:T(4,128)S(1)} %get-tuple-element.10.sent_ref), channel_id=1, source_target_pairs={{0,8},{8,16},{16,24},{1,9},{9,17},{17,25},{2,10},{10,18},{18,26},{... | collective-permute-start | bytes 3080 | tf_op jit(solution)/shard_map/ppermute | solution.py:171
  96.3 1.3 %collective-permute-start.9 = (f32[4,64]{1,0:T(4,128)S(1)}, f32[4,64]{1,0:T(4,128)S(1)}, u32[]{:S(2)}, u32[]{:S(2)}) collective-permute-start(f32[4,64]{1,0:T(4,128)S(1)} %get-tuple-element.10.sent_ref), channel_id=1, source_target_pairs={{8,0},{16,8},{24,16},{9,1},{17,9},{25,17},{10,2},{18,10},{26,18},{... | collective-permute-start | bytes 3080 | tf_op jit(solution)/shard_map/ppermute | solution.py:171
  97.6 0.7 pad_add_fusion.flags_ref
  98.3 0.6 copy.31.endpos_ref
  98.9 0.6 copy.38
  100.0 1.8 %collective-permute-done.9.after_ref = f32[4,64]{1,0:T(4,128)S(1)} collective-permute-done((f32[4,64]{1,0:T(4,128)S(1)}, f32[4,64]{1,0:T(4,128)S(1)}, u32[]{:S(2)}, u32[]{:S(2)}) %collective-permute-start.9) | collective-permute-done | bytes 1056 | tf_op jit(solution)/shard_map/ppermute | solution.py:171
  101.8 0.6 copy-done.6
  102.4 1.8 %project.1 = f32[3,1,64]{2,1,0:T(1,128)} custom-call(s32[4]{0:T(128)} %pad_add_fusion.flags_ref, f32[2]{0:T(128)} %ends_ref.1, f32[4,64]{1,0:T(4,128)} %copy-done.2, f32[4,64]{1,0:T(4,128)} %get-tuple-element.11.nl_ref, f32[3,64]{1,0:T(4,128)} %bitcast.46, f32[4,64]{1,0:T(4,128)} %copy-done.5, f32[4,64]{1,0:T(4,128)} %copy-done.6, f32[2,3,64]{2,1,0:T(4,128)} %copy.31.endpos_ref), custom_call_target="tpu_custom_call" | custom-call | tf_op jit(solution)/shard_map/project/pallas_call | solution.py:257
  (42 shorter events, 1.8 us)
Async XLA Ops:
  11.6 7.3 %collective-permute-start.1 = (f32[64,16384]{1,0:T(8,128)S(1)}, f32[64,16384]{1,0:T(8,128)S(1)}, u32[]{:S(2)}, u32[]{:S(2)}) collective-permute-start(f32[64,16384]{1,0:T(8,128)S(1)} %bitcast.43), channel_id=1, source_target_pairs={{0,4},{4,0},{1,5},{5,1},{2,6},{6,2},{3,7},{7,3},{8,12},{12,8},{9,1... | collective-permute-start | bytes 12582920 | tf_op jit(solution)/shard_map/ppermute | solution.py:268
  14.6 1.3 %copy-start.7 = (f32[1,3,64]{2,0,1:T(1,128)S(1)}, f32[1,3,64]{2,0,1:T(1,128)}, u32[]{:S(2)}) copy-start(f32[1,3,64]{2,0,1:T(1,128)} %param.21) | copy-start | bytes 2308
  14.6 28.7 %collective-permute-start = (f32[64,16384]{1,0:T(8,128)S(1)}, f32[64,16384]{1,0:T(8,128)}, u32[]{:S(2)}, u32[]{:S(2)}) collective-permute-start(f32[64,16384]{1,0:T(8,128)S(1)} %bitcast.42), channel_id=1, source_target_pairs={{0,4},{4,0},{1,5},{5,1},{2,6},{6,2},{3,7},{7,3},{8,12},{12,8},{9,1... | collective-permute-start | bytes 12582920 | tf_op jit(solution)/shard_map/ppermute | solution.py:268
  14.7 2.4 %copy-start.9 = (s32[4]{0:T(128)S(1)}, s32[4]{0:T(128)}, u32[]{:S(2)}) copy-start(s32[4]{0:T(128)} %param.19) | copy-start | bytes 52
  14.7 6.3 %copy-start = (s32[64]{0:T(128)S(1)}, s32[64]{0:T(128)}, u32[]{:S(2)}) copy-start(s32[64]{0:T(128)} %refs_0_.3) | copy-start | bytes 772
  14.7 6.3 %copy-start.1 = (f32[3,65536]{1,0:T(4,128)S(1)}, f32[3,65536]{1,0:T(4,128)}, u32[]{:S(2)}) copy-start(f32[3,65536]{1,0:T(4,128)} %refs_3_.3) | copy-start | bytes 2359300
  19.0 2.0 %copy-start.10 = (f32[64,16384]{1,0:T(8,128)}, f32[64,16384]{1,0:T(8,128)S(1)}, u32[]{:S(2)}) copy-start(f32[64,16384]{1,0:T(8,128)S(1)} %collective-permute-done.1.refs_7_) | copy-start | bytes 12582916
  43.3 26.9 %copy-start.4 = (f32[4,8]{1,0:T(4,128)S(1)}, f32[4,8]{1,0:T(4,128)}, u32[]{:S(2)}) copy-start(f32[4,8]{1,0:T(4,128)} %param.20) | copy-start | bytes 388
  43.3 54.9 %copy-start.3 = (f32[2,3,64]{2,0,1:T(2,128)S(1)}, f32[2,3,64]{2,0,1:T(2,128)}, u32[]{:S(2)}) copy-start(f32[2,3,64]{2,0,1:T(2,128)} %param.24) | copy-start | bytes 4612
  43.3 55.5 %copy-start.8 = (f32[1,3,64]{2,0,1:T(1,128)S(1)}, f32[1,3,64]{2,0,1:T(1,128)}, u32[]{:S(2)}) copy-start(f32[1,3,64]{2,0,1:T(1,128)} %param.23) | copy-start | bytes 2308
  65.5 1.6 %collective-permute-start.2 = (f32[512,128]{1,0:T(8,128)S(1)}, f32[512,128]{1,0:T(8,128)S(1)}, u32[]{:S(2)}, u32[]{:S(2)}) collective-permute-start(f32[512,128]{1,0:T(8,128)S(1)} %add.95), channel_id=1, source_target_pairs={{0,4},{4,0},{1,5},{5,1},{2,6},{6,2},{3,7},{7,3},{8,12},{12,8},{9,1... | collective-permute-start | bytes 786440 | tf_op jit(solution)/shard_map/ppermute | solution.py:268
  67.2 6.8 %collective-permute-start.3 = (f32[256,128]{1,0:T(8,128)S(1)}, f32[256,128]{1,0:T(8,128)S(1)}, u32[]{:S(2)}, u32[]{:S(2)}) collective-permute-start(f32[256,128]{1,0:T(8,128)S(1)} %constant_dynamic-slice_fusion.2), channel_id=1, source_target_pairs={{0,1},{1,0},{2,3},{3,2},{4,5},{5,4},{6,7},{7,6},{8,9},{9,8},{10,11... | collective-permute-start | bytes 393224 | tf_op jit(solution)/shard_map/ppermute | solution.py:268
  74.0 5.4 %collective-permute-start.4 = (f32[128,128]{1,0:T(8,128)S(1)}, f32[128,128]{1,0:T(8,128)S(1)}, u32[]{:S(2)}, u32[]{:S(2)}) collective-permute-start(f32[128,128]{1,0:T(8,128)S(1)} %constant_dynamic-slice_fusion.1), channel_id=1, source_target_pairs={{0,2},{1,3},{2,0},{3,1},{4,6},{5,7},{6,4},{7,5},{8,10},{9,11},{10,... | collective-permute-start | bytes 196616 | tf_op jit(solution)/shard_map/ppermute | solution.py:268
  82.0 1.4 %collective-permute-start.5 = (f32[4,64]{1,0:T(4,128)}, f32[4,64]{1,0:T(4,128)S(1)}, u32[]{:S(2)}, u32[]{:S(2)}) collective-permute-start(f32[4,64]{1,0:T(4,128)} %terms.1), channel_id=1, source_target_pairs={{0,4},{4,0},{1,5},{5,1},{2,6},{6,2},{3,7},{7,3},{8,12},{12,8},{9,1... | collective-permute-start | bytes 3080 | tf_op jit(solution)/shard_map/ppermute | solution.py:268
  84.1 3.6 %collective-permute-start.6 = (f32[4,64]{1,0:T(4,128)S(1)}, f32[4,64]{1,0:T(4,128)S(1)}, u32[]{:S(2)}, u32[]{:S(2)}) collective-permute-start(f32[4,64]{1,0:T(4,128)S(1)} %add.104), channel_id=1, source_target_pairs={{0,1},{1,0},{2,3},{3,2},{4,5},{5,4},{6,7},{7,6},{8,9},{9,8},{10,11... | collective-permute-start | bytes 3080 | tf_op jit(solution)/shard_map/ppermute | solution.py:268
  87.7 4.7 %collective-permute-start.7 = (f32[4,64]{1,0:T(4,128)S(1)}, f32[4,64]{1,0:T(4,128)S(1)}, u32[]{:S(2)}, u32[]{:S(2)}) collective-permute-start(f32[4,64]{1,0:T(4,128)S(1)} %add.105), channel_id=1, source_target_pairs={{0,2},{1,3},{2,0},{3,1},{4,6},{5,7},{6,4},{7,5},{8,10},{9,11},{10,... | collective-permute-start | bytes 3080 | tf_op jit(solution)/shard_map/ppermute | solution.py:268
  92.9 8.9 %copy-start.2 = (f32[4,64]{1,0:T(4,128)}, f32[4,64]{1,0:T(4,128)S(1)}, u32[]{:S(2)}) copy-start(f32[4,64]{1,0:T(4,128)S(1)} %get-tuple-element.10.sent_ref) | copy-start | bytes 3076
  92.9 7.1 %collective-permute-start.8 = (f32[4,64]{1,0:T(4,128)S(1)}, f32[4,64]{1,0:T(4,128)S(1)}, u32[]{:S(2)}, u32[]{:S(2)}) collective-permute-start(f32[4,64]{1,0:T(4,128)S(1)} %get-tuple-element.10.sent_ref), channel_id=1, source_target_pairs={{0,8},{8,16},{16,24},{1,9},{9,17},{17,25},{2,10},{10,18},{18,26},{... | collective-permute-start | bytes 3080 | tf_op jit(solution)/shard_map/ppermute | solution.py:171
  96.3 5.5 %collective-permute-start.9 = (f32[4,64]{1,0:T(4,128)S(1)}, f32[4,64]{1,0:T(4,128)S(1)}, u32[]{:S(2)}, u32[]{:S(2)}) collective-permute-start(f32[4,64]{1,0:T(4,128)S(1)} %get-tuple-element.10.sent_ref), channel_id=1, source_target_pairs={{8,0},{16,8},{24,16},{9,1},{17,9},{25,17},{10,2},{18,10},{26,18},{... | collective-permute-start | bytes 3080 | tf_op jit(solution)/shard_map/ppermute | solution.py:171
  100.0 1.8 %copy-start.5 = (f32[4,64]{1,0:T(4,128)}, f32[4,64]{1,0:T(4,128)S(1)}, u32[]{:S(2)}) copy-start(f32[4,64]{1,0:T(4,128)S(1)} %collective-permute-done.8.before_ref) | copy-start | bytes 3076
  101.8 0.6 copy-start.6

commit v5 on v4

--- a/solution.py
+++ b/solution.py
@@ -123,7 +123,8 @@
             outs[k][...] = 2.0 * acc[:, k * cols : (k + 1) * cols]
 
 
-def contract(sp, start, waves, ff, g, posb, live, gc=1024, blk=4096, rb=256):
+def contract(sp, start, waves, ff, g, posb, live, gc=2048, blk=4096, rb=256):
+    gc = min(gc, blk // 2)
     nspec, pmax, _ = ff.shape
     atoms = posb.shape[1]
     parts = len(waves)

time: 104 us -> 102 us (0.981)
  Pallas kernels: 48.1 us -> 46.2 us
    pallas_call x2, Pallas kernels: 44.3 us -> 42.5 us  [contract(): pl.pallas_call(functools.partial(contract_kernel, parts=parts, gc=gc, rb=...]
where the time goes in v5:
time: 102 us
  Pallas kernels  46.2 us (45%)
  starting transfers between devices  15.8 us (15%)
  waiting for transfers between devices  13.6 us (13%)
  local copies, waits for them, and re-layouts  12.4 us (12%)
  other arithmetic  11.3 us (11%)
  between operations  2.86 us (3%)
    pallas_call x2, Pallas kernels, contract(): pl.pallas_call(functools.partial(contract_kernel, parts=parts, gc=gc, rb=...  42.5 us
    ppermute x8, waiting for transfers between devices, swapped(): return lax.ppermute(array, axis, pairs)  11.8 us
    ppermute x8, starting transfers between devices, swapped(): return lax.ppermute(array, axis, pairs)  11.2 us
    convert_element_type x1, other arithmetic, per_device(): given = rows_of((1 - core) * half + at, count).astype(jnp.float32)  8.51 us
    unnamed x27, local copies, waits for them, and re-layouts  6.04 us
    convert_element_type x2, local copies, waits for them, and re-layouts, per_device(): given = rows_of((1 - core) * half + at, count).astype(jnp.float32)  4.86 us
    ppermute x2, starting transfers between devices, passed_along(): return lax.ppermute(array, axis, pairs)  4.68 us
  transfers between devices with their start and end apart: 10, of which 7 were waited for; matrix products, arithmetic and copies ran while one was open for 8% of the time, Pallas kernels for 21%

profile of v5, /device:TPU:0, one launch (start us, length us, event | category | flops | bytes accessed | tf_op | source)
XLA Modules:
  0.0 102.3 jit_solution(17572252526693645857)
XLA Ops:
  0.7 8.5 %convert_bitcast_fusion = (f32[2,32,16384]{2,0,1:T(2,128)S(1)}, bf16[1,32,2,16384]{3,2,1,0:T(2,128)(2,1)S(1)}, bf16[1,32,2,16384]{3,2,1,0:T(2,128)(2,1)S(1)}, f32[2,32,16384]{2,0,1:T(2,128)S(1)}) fusion(bf16[1,32,2,65536]{3,2,1,0:T(2,128)(2,1)} %param.14, s32[]{:T(128)S(6)} %select_n.58, s32[]{:T(128)S(6)} %select_n.55, s32[]{:T(128)S(6)} %select_n.57, ...), kind=kLoop, calls=%fused_computation | loop fusion | flops 2097152 | bytes 20971536 | tf_op jit(solution)/shard_map/convert_element_type | solution.py:334
  9.2 2.4 %copy.28 = f32[2,32,16384]{2,1,0:T(8,128)S(1)} copy(f32[2,32,16384]{2,0,1:T(2,128)S(1)} %get-tuple-element.12) | data formatting | bytes 8388608 | tf_op jit(solution)/shard_map/convert_element_type | solution.py:334
  11.6 0.6 collective-permute-start.1
  12.2 2.4 %copy.26 = f32[2,32,16384]{2,1,0:T(8,128)S(1)} copy(f32[2,32,16384]{2,0,1:T(2,128)S(1)} %get-tuple-element.15) | data formatting | bytes 8388608 | tf_op jit(solution)/shard_map/convert_element_type | solution.py:334
  14.7 1.2 %copy.35 = bf16[1,32,2,16384]{3,1,2,0:T(8,128)(2,1)S(1)} copy(bf16[1,32,2,16384]{3,2,1,0:T(2,128)(2,1)S(1)} %get-tuple-element.14) | data formatting | bytes 4194304
  15.9 1.2 %copy.34 = bf16[1,32,2,16384]{3,1,2,0:T(8,128)(2,1)S(1)} copy(bf16[1,32,2,16384]{3,2,1,0:T(2,128)(2,1)S(1)} %get-tuple-element.13) | data formatting | bytes 4194304
  17.2 1.8 %collective-permute-done.1.refs_7_ = f32[64,16384]{1,0:T(8,128)S(1)} collective-permute-done((f32[64,16384]{1,0:T(8,128)S(1)}, f32[64,16384]{1,0:T(8,128)S(1)}, u32[]{:S(2)}, u32[]{:S(2)}) %collective-permute-start.1) | collective-permute-done | bytes 4194336 | tf_op jit(solution)/shard_map/ppermute | solution.py:269
  19.1 1.9 %copy-done.10 = f32[64,16384]{1,0:T(8,128)} copy-done((f32[64,16384]{1,0:T(8,128)}, f32[64,16384]{1,0:T(8,128)S(1)}, u32[]{:S(2)}) %copy-start.10) | copy-done | bytes 4194328
  21.0 21.3 %contract.3 = (f32[512,128]{1,0:T(8,128)S(1)}, f32[512,128]{1,0:T(8,128)S(1)}) custom-call(s32[64]{0:T(128)S(1)} %copy-done, s32[1]{0:T(128)} %bitcast.12.refs_1_, f32[4,8,65536]{2,1,0:T(8,128)} %refs_2_.3, f32[3,65536]{1,0:T(4,128)S(1)} %copy-done.1, f32[3,64,128]{2,1,0:T(8,128)S(1)} %broadcast_in_dim.15.refs_4_, ...), custom_call_target="tpu_custom_call" | custom-call | flops 8589934592 | bytes 4587520 | tf_op jit(solution)/shard_map/contract/pallas_call | solution.py:139
  42.4 21.1 %contract.2 = (f32[512,128]{1,0:T(8,128)S(1)}, f32[512,128]{1,0:T(8,128)S(1)}) custom-call(s32[64]{0:T(128)S(1)} %copy-done, s32[1]{0:T(128)} %bitcast.5.refs_1_, f32[4,8,65536]{2,1,0:T(8,128)} %refs_2_.3, f32[3,65536]{1,0:T(4,128)S(1)} %copy-done.1, f32[3,64,128]{2,1,0:T(8,128)S(1)} %broadcast_in_dim.15.refs_4_, f32[4,8,128]{2,1,0:T(8,128)S(1)} %broadcast_in_dim.16.refs_5_, ...), custom_call_target="tpu_custom_call" | custom-call | flops 8589934592 | bytes 4587520 | tf_op jit(solution)/shard_map/contract/pallas_call | solution.py:139
  64.0 1.2 %collective-permute-done.2 = f32[512,128]{1,0:T(8,128)S(1)} collective-permute-done((f32[512,128]{1,0:T(8,128)S(1)}, f32[512,128]{1,0:T(8,128)S(1)}, u32[]{:S(2)}, u32[]{:S(2)}) %collective-permute-start.2) | collective-permute-done | bytes 262176 | tf_op jit(solution)/shard_map/ppermute | solution.py:269
  65.3 3.0 %collective-permute-start.3 = (f32[256,128]{1,0:T(8,128)S(1)}, f32[256,128]{1,0:T(8,128)S(1)}, u32[]{:S(2)}, u32[]{:S(2)}) collective-permute-start(f32[256,128]{1,0:T(8,128)S(1)} %constant_dynamic-slice_fusion.2), channel_id=1, source_target_pairs={{0,1},{1,0},{2,3},{3,2},{4,5},{5,4},{6,7},{7,6},{8,9},{9,8},{10,11... | collective-permute-start | bytes 393224 | tf_op jit(solution)/shard_map/ppermute | solution.py:269
  68.6 3.5 %collective-permute-done.3 = f32[256,128]{1,0:T(8,128)S(1)} collective-permute-done((f32[256,128]{1,0:T(8,128)S(1)}, f32[256,128]{1,0:T(8,128)S(1)}, u32[]{:S(2)}, u32[]{:S(2)}) %collective-permute-start.3) | collective-permute-done | bytes 131104 | tf_op jit(solution)/shard_map/ppermute | solution.py:269
  72.1 2.8 %collective-permute-start.4 = (f32[128,128]{1,0:T(8,128)S(1)}, f32[128,128]{1,0:T(8,128)S(1)}, u32[]{:S(2)}, u32[]{:S(2)}) collective-permute-start(f32[128,128]{1,0:T(8,128)S(1)} %constant_dynamic-slice_fusion.1), channel_id=1, source_target_pairs={{0,2},{1,3},{2,0},{3,1},{4,6},{5,7},{6,4},{7,5},{8,10},{9,11},{10,... | collective-permute-start | bytes 196616 | tf_op jit(solution)/shard_map/ppermute | solution.py:269
  74.9 0.6 constant_dynamic-slice_fusion.strength_ref
  75.6 2.0 %collective-permute-done.4 = f32[128,128]{1,0:T(8,128)S(1)} collective-permute-done((f32[128,128]{1,0:T(8,128)S(1)}, f32[128,128]{1,0:T(8,128)S(1)}, u32[]{:S(2)}, u32[]{:S(2)}) %collective-permute-start.4) | collective-permute-done | bytes 65568 | tf_op jit(solution)/shard_map/ppermute | solution.py:269
  77.5 0.6 dynamic-slice_add_fusion.1.sums_ref
  78.2 1.9 %terms.1 = f32[4,64]{1,0:T(4,128)} custom-call(s32[1]{0:T(128)} %bitcast.4.first_ref, f32[128,128]{1,0:T(8,128)} %dynamic-slice_add_fusion.1.sums_ref, f32[1,32]{1,0:T(1,128)} %occ_ref.1, f32[128,1]{1,0:T(8,128)} %constant_dynamic-slice_fusion.strength_ref), custom_call_target="tpu_custom_call" | custom-call | tf_op jit(solution)/shard_map/terms/pallas_call | solution.py:206
  80.1 1.4 %collective-permute-done.5 = f32[4,64]{1,0:T(4,128)S(1)} collective-permute-done((f32[4,64]{1,0:T(4,128)}, f32[4,64]{1,0:T(4,128)S(1)}, u32[]{:S(2)}, u32[]{:S(2)}) %collective-permute-start.5) | collective-permute-done | bytes 1056 | tf_op jit(solution)/shard_map/ppermute | solution.py:269
  81.5 0.7 add.104
  82.2 1.6 %collective-permute-start.6 = (f32[4,64]{1,0:T(4,128)S(1)}, f32[4,64]{1,0:T(4,128)S(1)}, u32[]{:S(2)}, u32[]{:S(2)}) collective-permute-start(f32[4,64]{1,0:T(4,128)S(1)} %add.104), channel_id=1, source_target_pairs={{0,1},{1,0},{2,3},{3,2},{4,5},{5,4},{6,7},{7,6},{8,9},{9,8},{10,11... | collective-permute-start | bytes 3080 | tf_op jit(solution)/shard_map/ppermute | solution.py:269
  83.7 2.0 %collective-permute-done.6 = f32[4,64]{1,0:T(4,128)S(1)} collective-permute-done((f32[4,64]{1,0:T(4,128)S(1)}, f32[4,64]{1,0:T(4,128)S(1)}, u32[]{:S(2)}, u32[]{:S(2)}) %collective-permute-start.6) | collective-permute-done | bytes 1056 | tf_op jit(solution)/shard_map/ppermute | solution.py:269
  85.8 2.7 %collective-permute-start.7 = (f32[4,64]{1,0:T(4,128)S(1)}, f32[4,64]{1,0:T(4,128)S(1)}, u32[]{:S(2)}, u32[]{:S(2)}) collective-permute-start(f32[4,64]{1,0:T(4,128)S(1)} %add.105), channel_id=1, source_target_pairs={{0,2},{1,3},{2,0},{3,1},{4,6},{5,7},{6,4},{7,5},{8,10},{9,11},{10,... | collective-permute-start | bytes 3080 | tf_op jit(solution)/shard_map/ppermute | solution.py:269
  90.4 0.6 pad_select_fusion
  91.0 3.4 %collective-permute-start.8 = (f32[4,64]{1,0:T(4,128)S(1)}, f32[4,64]{1,0:T(4,128)S(1)}, u32[]{:S(2)}, u32[]{:S(2)}) collective-permute-start(f32[4,64]{1,0:T(4,128)S(1)} %get-tuple-element.10.sent_ref), channel_id=1, source_target_pairs={{0,8},{8,16},{16,24},{1,9},{9,17},{17,25},{2,10},{10,18},{18,26},{... | collective-permute-start | bytes 3080 | tf_op jit(solution)/shard_map/ppermute | solution.py:172
  94.4 1.3 %collective-permute-start.9 = (f32[4,64]{1,0:T(4,128)S(1)}, f32[4,64]{1,0:T(4,128)S(1)}, u32[]{:S(2)}, u32[]{:S(2)}) collective-permute-start(f32[4,64]{1,0:T(4,128)S(1)} %get-tuple-element.10.sent_ref), channel_id=1, source_target_pairs={{8,0},{16,8},{24,16},{9,1},{17,9},{25,17},{10,2},{18,10},{26,18},{... | collective-permute-start | bytes 3080 | tf_op jit(solution)/shard_map/ppermute | solution.py:172
  95.7 0.7 pad_add_fusion.flags_ref
  96.4 0.6 copy.31.endpos_ref
  97.0 0.6 copy.38
  98.1 1.8 %collective-permute-done.9.after_ref = f32[4,64]{1,0:T(4,128)S(1)} collective-permute-done((f32[4,64]{1,0:T(4,128)S(1)}, f32[4,64]{1,0:T(4,128)S(1)}, u32[]{:S(2)}, u32[]{:S(2)}) %collective-permute-start.9) | collective-permute-done | bytes 1056 | tf_op jit(solution)/shard_map/ppermute | solution.py:172
  99.9 0.6 copy-done.6
  100.5 1.8 %project.1 = f32[3,1,64]{2,1,0:T(1,128)} custom-call(s32[4]{0:T(128)} %pad_add_fusion.flags_ref, f32[2]{0:T(128)} %ends_ref.1, f32[4,64]{1,0:T(4,128)} %copy-done.2, f32[4,64]{1,0:T(4,128)} %get-tuple-element.11.nl_ref, f32[3,64]{1,0:T(4,128)} %bitcast.46, f32[4,64]{1,0:T(4,128)} %copy-done.5, f32[4,64]{1,0:T(4,128)} %copy-done.6, f32[2,3,64]{2,1,0:T(4,128)} %copy.31.endpos_ref), custom_call_target="tpu_custom_call" | custom-call | tf_op jit(solution)/shard_map/project/pallas_call | solution.py:258
  (42 shorter events, 1.7 us)
Async XLA Ops:
  11.6 7.3 %collective-permute-start.1 = (f32[64,16384]{1,0:T(8,128)S(1)}, f32[64,16384]{1,0:T(8,128)S(1)}, u32[]{:S(2)}, u32[]{:S(2)}) collective-permute-start(f32[64,16384]{1,0:T(8,128)S(1)} %bitcast.43), channel_id=1, source_target_pairs={{0,4},{4,0},{1,5},{5,1},{2,6},{6,2},{3,7},{7,3},{8,12},{12,8},{9,1... | collective-permute-start | bytes 12582920 | tf_op jit(solution)/shard_map/ppermute | solution.py:269
  14.6 1.3 %copy-start.7 = (f32[1,3,64]{2,0,1:T(1,128)S(1)}, f32[1,3,64]{2,0,1:T(1,128)}, u32[]{:S(2)}) copy-start(f32[1,3,64]{2,0,1:T(1,128)} %param.21) | copy-start | bytes 2308
  14.6 27.8 %collective-permute-start = (f32[64,16384]{1,0:T(8,128)S(1)}, f32[64,16384]{1,0:T(8,128)}, u32[]{:S(2)}, u32[]{:S(2)}) collective-permute-start(f32[64,16384]{1,0:T(8,128)S(1)} %bitcast.42), channel_id=1, source_target_pairs={{0,4},{4,0},{1,5},{5,1},{2,6},{6,2},{3,7},{7,3},{8,12},{12,8},{9,1... | collective-permute-start | bytes 12582920 | tf_op jit(solution)/shard_map/ppermute | solution.py:269
  14.7 2.4 %copy-start.9 = (s32[4]{0:T(128)S(1)}, s32[4]{0:T(128)}, u32[]{:S(2)}) copy-start(s32[4]{0:T(128)} %param.19) | copy-start | bytes 52
  14.7 6.3 %copy-start = (s32[64]{0:T(128)S(1)}, s32[64]{0:T(128)}, u32[]{:S(2)}) copy-start(s32[64]{0:T(128)} %refs_0_.3) | copy-start | bytes 772
  14.7 6.3 %copy-start.1 = (f32[3,65536]{1,0:T(4,128)S(1)}, f32[3,65536]{1,0:T(4,128)}, u32[]{:S(2)}) copy-start(f32[3,65536]{1,0:T(4,128)} %refs_3_.3) | copy-start | bytes 2359300
  19.0 2.0 %copy-start.10 = (f32[64,16384]{1,0:T(8,128)}, f32[64,16384]{1,0:T(8,128)S(1)}, u32[]{:S(2)}) copy-start(f32[64,16384]{1,0:T(8,128)S(1)} %collective-permute-done.1.refs_7_) | copy-start | bytes 12582916
  42.4 25.9 %copy-start.4 = (f32[4,8]{1,0:T(4,128)S(1)}, f32[4,8]{1,0:T(4,128)}, u32[]{:S(2)}) copy-start(f32[4,8]{1,0:T(4,128)} %param.20) | copy-start | bytes 388
  42.4 54.0 %copy-start.3 = (f32[2,3,64]{2,0,1:T(2,128)S(1)}, f32[2,3,64]{2,0,1:T(2,128)}, u32[]{:S(2)}) copy-start(f32[2,3,64]{2,0,1:T(2,128)} %param.24) | copy-start | bytes 4612
  42.4 54.6 %copy-start.8 = (f32[1,3,64]{2,0,1:T(1,128)S(1)}, f32[1,3,64]{2,0,1:T(1,128)}, u32[]{:S(2)}) copy-start(f32[1,3,64]{2,0,1:T(1,128)} %param.23) | copy-start | bytes 2308
  63.6 1.6 %collective-permute-start.2 = (f32[512,128]{1,0:T(8,128)S(1)}, f32[512,128]{1,0:T(8,128)S(1)}, u32[]{:S(2)}, u32[]{:S(2)}) collective-permute-start(f32[512,128]{1,0:T(8,128)S(1)} %add.95), channel_id=1, source_target_pairs={{0,4},{4,0},{1,5},{5,1},{2,6},{6,2},{3,7},{7,3},{8,12},{12,8},{9,1... | collective-permute-start | bytes 786440 | tf_op jit(solution)/shard_map/ppermute | solution.py:269
  65.3 6.8 %collective-permute-start.3 = (f32[256,128]{1,0:T(8,128)S(1)}, f32[256,128]{1,0:T(8,128)S(1)}, u32[]{:S(2)}, u32[]{:S(2)}) collective-permute-start(f32[256,128]{1,0:T(8,128)S(1)} %constant_dynamic-slice_fusion.2), channel_id=1, source_target_pairs={{0,1},{1,0},{2,3},{3,2},{4,5},{5,4},{6,7},{7,6},{8,9},{9,8},{10,11... | collective-permute-start | bytes 393224 | tf_op jit(solution)/shard_map/ppermute | solution.py:269
  72.1 5.4 %collective-permute-start.4 = (f32[128,128]{1,0:T(8,128)S(1)}, f32[128,128]{1,0:T(8,128)S(1)}, u32[]{:S(2)}, u32[]{:S(2)}) collective-permute-start(f32[128,128]{1,0:T(8,128)S(1)} %constant_dynamic-slice_fusion.1), channel_id=1, source_target_pairs={{0,2},{1,3},{2,0},{3,1},{4,6},{5,7},{6,4},{7,5},{8,10},{9,11},{10,... | collective-permute-start | bytes 196616 | tf_op jit(solution)/shard_map/ppermute | solution.py:269
  80.1 1.4 %collective-permute-start.5 = (f32[4,64]{1,0:T(4,128)}, f32[4,64]{1,0:T(4,128)S(1)}, u32[]{:S(2)}, u32[]{:S(2)}) collective-permute-start(f32[4,64]{1,0:T(4,128)} %terms.1), channel_id=1, source_target_pairs={{0,4},{4,0},{1,5},{5,1},{2,6},{6,2},{3,7},{7,3},{8,12},{12,8},{9,1... | collective-permute-start | bytes 3080 | tf_op jit(solution)/shard_map/ppermute | solution.py:269
  82.2 3.6 %collective-permute-start.6 = (f32[4,64]{1,0:T(4,128)S(1)}, f32[4,64]{1,0:T(4,128)S(1)}, u32[]{:S(2)}, u32[]{:S(2)}) collective-permute-start(f32[4,64]{1,0:T(4,128)S(1)} %add.104), channel_id=1, source_target_pairs={{0,1},{1,0},{2,3},{3,2},{4,5},{5,4},{6,7},{7,6},{8,9},{9,8},{10,11... | collective-permute-start | bytes 3080 | tf_op jit(solution)/shard_map/ppermute | solution.py:269
  85.8 4.7 %collective-permute-start.7 = (f32[4,64]{1,0:T(4,128)S(1)}, f32[4,64]{1,0:T(4,128)S(1)}, u32[]{:S(2)}, u32[]{:S(2)}) collective-permute-start(f32[4,64]{1,0:T(4,128)S(1)} %add.105), channel_id=1, source_target_pairs={{0,2},{1,3},{2,0},{3,1},{4,6},{5,7},{6,4},{7,5},{8,10},{9,11},{10,... | collective-permute-start | bytes 3080 | tf_op jit(solution)/shard_map/ppermute | solution.py:269
  91.0 8.9 %copy-start.2 = (f32[4,64]{1,0:T(4,128)}, f32[4,64]{1,0:T(4,128)S(1)}, u32[]{:S(2)}) copy-start(f32[4,64]{1,0:T(4,128)S(1)} %get-tuple-element.10.sent_ref) | copy-start | bytes 3076
  91.0 7.1 %collective-permute-start.8 = (f32[4,64]{1,0:T(4,128)S(1)}, f32[4,64]{1,0:T(4,128)S(1)}, u32[]{:S(2)}, u32[]{:S(2)}) collective-permute-start(f32[4,64]{1,0:T(4,128)S(1)} %get-tuple-element.10.sent_ref), channel_id=1, source_target_pairs={{0,8},{8,16},{16,24},{1,9},{9,17},{17,25},{2,10},{10,18},{18,26},{... | collective-permute-start | bytes 3080 | tf_op jit(solution)/shard_map/ppermute | solution.py:172
  94.4 5.5 %collective-permute-start.9 = (f32[4,64]{1,0:T(4,128)S(1)}, f32[4,64]{1,0:T(4,128)S(1)}, u32[]{:S(2)}, u32[]{:S(2)}) collective-permute-start(f32[4,64]{1,0:T(4,128)S(1)} %get-tuple-element.10.sent_ref), channel_id=1, source_target_pairs={{8,0},{16,8},{24,16},{9,1},{17,9},{25,17},{10,2},{18,10},{26,18},{... | collective-permute-start | bytes 3080 | tf_op jit(solution)/shard_map/ppermute | solution.py:172
  98.1 1.8 %copy-start.5 = (f32[4,64]{1,0:T(4,128)}, f32[4,64]{1,0:T(4,128)S(1)}, u32[]{:S(2)}) copy-start(f32[4,64]{1,0:T(4,128)S(1)} %collective-permute-done.8.before_ref) | copy-start | bytes 3076
  99.9 0.6 copy-start.6
